TPU v7x, 256 devices: a whole 4x4x8 slice. The times are simulated.
256 devices in a mesh: seq: 32 (over y, z), head: 8 (over x, core).
Axes of the slice: x: 4, y: 4, z: 8, core: 2. Of those that a mesh axis runs over, the one named last changes fastest.
Arguments:
- queries: float32 [4096, 32, 128], P('seq', 'head'), may hold values from -0.6 to 0.6
- keys: float32 [4096, 32, 128], P('seq', 'head'), may hold values from -0.6 to 0.6
- values: float32 [4096, 32, 128], P('seq', 'head'), may hold values from -6 to 6
- level_weights: float32 [7, 32, 4096], P(None, 'head', 'seq'), may hold values from 0.02 to 0.2
- out_proj: bfloat16 [4096, 4096], P('head'), may hold values from -0.125 to 0.125
- out_grad: bfloat16 [4096, 4096], P('seq', 'head'), may hold values from -6 to 6
Outputs:
- mixed: bfloat16 [4096, 4096], P('seq', 'head')
- query_grad: float32 [4096, 32, 128], P('seq', 'head')
- key_grad: float32 [4096, 32, 128], P('seq', 'head')
- value_grad: float32 [4096, 32, 128], P('seq', 'head')
- proj_grad: float32 [4096, 4096], P('head', 'seq')
All inputs are finite; a program needn't handle non-finite values.
Results may differ from a plain program's by a relative error of at most 0.015.
Values may be sent and summed in bfloat16 or wider, within the bound.
A program may use at most 64 MiB of HBM per device.

v0:
```python
import jax
import jax.numpy as jnp
from jax import lax
from jax.sharding import PartitionSpec as P

CH = 64


def swapped(block, axis, stride):
    count = lax.axis_size(axis)
    route = []
    for low in range(count):
        high = low | 1 << stride
        if high != low and high < count:
            route += [(low, high), (high, low)]
    return lax.ppermute(block, axis, route)


def body(queries, keys, values, level_weights, out_proj, out_grad):
    highest = lax.Precision.HIGHEST
    rows, heads_dev, head_dim = queries.shape
    local_bits = (rows // CH).bit_length() - 1
    seq_bits = lax.axis_size("seq").bit_length() - 1
    grad_full = lax.all_gather(out_grad, "head", axis=1, tiled=True)
    grad_heads = lax.dot_general(
        grad_full, out_proj, (((1,), (1,)), ((), ())), preferred_element_type=jnp.float32
    )
    grad_heads = grad_heads.reshape(rows, heads_dev, head_dim)
    weights_rows = jnp.transpose(level_weights, (0, 2, 1))
    position = jnp.arange(rows, dtype=jnp.int32)
    stretch_index = position // CH
    differ = stretch_index[:, None] ^ stretch_index[None, :]
    digit = 0
    level = (differ >= 1 << digit).astype(jnp.int32)
    causal = position[:, None] >= position[None, :]
    pair_weight = jnp.zeros((heads_dev, rows, rows), jnp.float32)
    for depth in range(local_bits + 1):
        pair_weight = pair_weight + jnp.where(
            (level == depth) & causal, level_weights[depth][:, :, None], 0.0
        )
    scores = jnp.einsum("thd,shd->hts", queries, keys, precision=highest)
    probs = scores * pair_weight
    attended_f = jnp.einsum("hts,shd->thd", probs, values, precision=highest)
    dprobs = jnp.einsum("thd,shd->hts", grad_heads, values, precision=highest) * pair_weight
    query_grad = jnp.einsum("hts,shd->thd", dprobs, keys, precision=highest)
    key_grad = jnp.einsum("hts,thd->shd", dprobs, queries, precision=highest)
    value_grad = jnp.einsum("hts,thd->shd", probs, grad_heads, precision=highest)
    key_state = jnp.einsum("shd,she->hde", keys, values, precision=highest)
    grad_states = jnp.stack(
        [
            jnp.einsum(
                "thd,the->hde",
                queries * weights_rows[1 + local_bits + digit][:, :, None],
                grad_heads,
                precision=highest,
            )
            for digit in range(seq_bits)
        ]
    )
    partner_keys = []
    partner_grads = []
    running = key_state
    pending = grad_states
    for digit in range(seq_bits):
        arrived = swapped(running, "seq", digit)
        partner_keys.append(arrived)
        running = running + arrived
    for digit in range(seq_bits):
        landed = swapped(pending, "seq", digit)
        partner_grads.append(landed[0])
        pending = pending[1:] + landed[1:]
    seq_place = lax.axis_index("seq")
    for digit in range(seq_bits):
        upper = (seq_place >> digit & 1).astype(jnp.float32)
        lower = 1.0 - upper
        level_scale = weights_rows[1 + local_bits + digit][:, :, None]
        attended_f = attended_f + upper * level_scale * jnp.einsum(
            "thd,hde->the", queries, partner_keys[digit], precision=highest
        )
        query_grad = query_grad + upper * level_scale * jnp.einsum(
            "the,hde->thd", grad_heads, partner_keys[digit], precision=highest
        )
        key_grad = key_grad + lower * jnp.einsum(
            "the,hde->thd", values, partner_grads[digit], precision=highest
        )
        value_grad = value_grad + lower * jnp.einsum(
            "thd,hde->the", keys, partner_grads[digit], precision=highest
        )
    attended = attended_f.reshape(rows, heads_dev * head_dim).astype(jnp.bfloat16)
    mixed = lax.psum_scatter(
        lax.dot_general(
            out_proj, attended, (((0,), (1,)), ((), ())), preferred_element_type=jnp.float32
        ),
        "head",
        scatter_dimension=0,
        tiled=True,
    ).T.astype(jnp.bfloat16)
    proj_grad = (
        lax.psum_scatter(
            lax.dot_general(
                grad_full, attended, (((0,), (0,)), ((), ())), preferred_element_type=jnp.float32
            ).astype(jnp.bfloat16),
            "seq",
            scatter_dimension=0,
            tiled=True,
        )
        .astype(jnp.float32)
        .T
    )
    return (mixed, query_grad, key_grad, value_grad, proj_grad)


def solution(mesh):
    placed = (
        P("seq", "head", None),
        P("seq", "head", None),
        P("seq", "head", None),
        P(None, "head", "seq"),
        P("head", None),
        P("seq", "head"),
    )
    return jax.shard_map(
        body,
        mesh=mesh,
        in_specs=placed,
        out_specs=(
            P("seq", "head"),
            P("seq", "head", None),
            P("seq", "head", None),
            P("seq", "head", None),
            P("head", "seq"),
        ),
        check_vma=False,
    )
```

profile of v0, /device:TPU:8, one launch (start us, length us, event | category | flops | bytes accessed | tf_op | source)
XLA Modules:
  0.0 372.4 jit_solution(5586583986697725850)
XLA Ops:
  7.2 0.9 copy-done
  8.1 1.5 fusion.60
  9.7 2.0 collective-permute-start
  11.8 0.7 slice_bitcast_fusion.18
  12.5 5.5 %collective-permute-done = f32[4,128,128]{2,1,0:T(8,128)S(1)} collective-permute-done((f32[4,128,128]{2,1,0:T(8,128)S(1)}, f32[4,128,128]{2,1,0:T(8,128)S(1)}, u32[]{:S(2)}, u32[]{:S(2)}) %collective-permute-start) | collective-permute-done | bytes 262176 | tf_op jit(solution)/shard_map/ppermute | solution.py:16
  18.0 3.4 collective-permute-start.1
  21.5 11.1 %collective-permute-done.1 = f32[4,128,128]{2,1,0:T(8,128)S(1)} collective-permute-done((f32[4,128,128]{2,1,0:T(8,128)S(1)}, f32[4,128,128]{2,1,0:T(8,128)S(1)}, u32[]{:S(2)}, u32[]{:S(2)}) %collective-permute-start.1) | collective-permute-done | bytes 262176 | tf_op jit(solution)/shard_map/ppermute | solution.py:16
  32.7 6.3 %collective-permute-start.2 = (f32[4,128,128]{2,1,0:T(8,128)S(1)}, f32[4,128,128]{2,1,0:T(8,128)S(1)}, u32[]{:S(2)}, u32[]{:S(2)}) collective-permute-start(f32[4,128,128]{2,1,0:T(8,128)S(1)} %add.109), channel_id=1, source_target_pairs={{0,32},{32,0},{8,40},{40,8},{16,48},{48,16},{24,56},{56,24},{64,96... | collective-permute-start | bytes 786440 | tf_op jit(solution)/shard_map/ppermute | solution.py:16
  39.0 0.7 convolution_multiply_fusion.11
  40.2 10.5 %collective-permute-done.2 = f32[4,128,128]{2,1,0:T(8,128)S(1)} collective-permute-done((f32[4,128,128]{2,1,0:T(8,128)S(1)}, f32[4,128,128]{2,1,0:T(8,128)S(1)}, u32[]{:S(2)}, u32[]{:S(2)}) %collective-permute-start.2) | collective-permute-done | bytes 262176 | tf_op jit(solution)/shard_map/ppermute | solution.py:16
  51.9 5.9 %collective-permute-done.3 = f32[4,128,128]{2,1,0:T(8,128)S(1)} collective-permute-done((f32[4,128,128]{2,1,0:T(8,128)S(1)}, f32[4,128,128]{2,1,0:T(8,128)S(1)}, u32[]{:S(2)}, u32[]{:S(2)}) %collective-permute-start.3) | collective-permute-done | bytes 262176 | tf_op jit(solution)/shard_map/ppermute | solution.py:16
  57.8 4.3 %collective-permute-start.4 = (f32[4,128,128]{2,1,0:T(8,128)S(1)}, f32[4,128,128]{2,1,0:T(8,128)S(1)}, u32[]{:S(2)}, u32[]{:S(2)}) collective-permute-start(f32[4,128,128]{2,1,0:T(8,128)S(1)} %add.113), channel_id=1, source_target_pairs={{0,128},{128,0},{8,136},{136,8},{16,144},{144,16},{24,152},{152,24... | collective-permute-start | bytes 786440 | tf_op jit(solution)/shard_map/ppermute | solution.py:16
  63.3 3.1 collective-permute-done.4
  67.8 2.1 convolution_bitcast_fusion
  70.7 1.6 broadcast_multiply_fusion
  72.4 4.5 %fusion = bf16[4096,512]{0,1:T(8,128)(2,1)} fusion(bf16[128,512]{0,1:T(8,128)(2,1)S(1)} %bitcast.204, bf16[128,4096]{1,0:T(8,128)(2,1)} %all-gather.2.cloned.1.call-done), kind=kOutput, calls=%fused_computation.1 | convolution fusion | flops 538968064 | bytes 5373952 | tf_op jit(solution)/shard_map/dot_general | solution.py:100
  76.9 6.5 %copy.176 = bf16[4096,512]{1,0:T(8,128)(2,1)} copy(bf16[4096,512]{0,1:T(8,128)(2,1)} %fusion) | data formatting | bytes 8388608
  83.4 1.2 copy-done.4
  84.6 3.6 fusion.72
  88.2 1.3 fusion.14
  89.5 1.3 constant_dynamic-update-slice_fusion.3
  90.8 1.3 constant_dynamic-update-slice_fusion.2
  92.1 1.3 constant_dynamic-update-slice_fusion.1
  93.4 1.4 constant_dynamic-update-slice_fusion
  95.8 24.3 %collective-permute-done.5 = f32[5,4,128,128]{3,2,1,0:T(8,128)} collective-permute-done((f32[5,4,128,128]{3,2,1,0:T(8,128)}, f32[5,4,128,128]{3,2,1,0:T(8,128)}, u32[]{:S(2)}, u32[]{:S(2)}) %collective-permute-start.5) | collective-permute-done | bytes 1310752 | tf_op jit(solution)/shard_map/ppermute | solution.py:16
  120.1 1.4 slice_add_fusion
  121.6 5.6 %collective-permute-start.6 = (f32[4,4,128,128]{3,2,1,0:T(8,128)S(1)}, f32[4,4,128,128]{3,2,1,0:T(8,128)S(1)}, u32[]{:S(2)}, u32[]{:S(2)}) collective-permute-start(f32[4,4,128,128]{3,2,1,0:T(8,128)S(1)} %slice_add_fusion), channel_id=1, source_target_pairs={{0,16},{16,0},{8,24},{24,8},{32,48},{48,32},{40,56},{56,40},{64,80... | collective-permute-start | bytes 3145736 | tf_op jit(solution)/shard_map/ppermute | solution.py:16
  128.9 1.1 fusion.34
  130.1 46.1 %collective-permute-done.6 = f32[4,4,128,128]{3,2,1,0:T(8,128)S(1)} collective-permute-done((f32[4,4,128,128]{3,2,1,0:T(8,128)S(1)}, f32[4,4,128,128]{3,2,1,0:T(8,128)S(1)}, u32[]{:S(2)}, u32[]{:S(2)}) %collective-permute-start.6) | collective-permute-done | bytes 1048608 | tf_op jit(solution)/shard_map/ppermute | solution.py:16
  176.3 0.9 copy-done.5
  177.2 6.1 %collective-permute-start.7 = (f32[3,4,128,128]{3,2,1,0:T(8,128)S(1)}, f32[3,4,128,128]{3,2,1,0:T(8,128)S(1)}, u32[]{:S(2)}, u32[]{:S(2)}) collective-permute-start(f32[3,4,128,128]{3,2,1,0:T(8,128)S(1)} %slice_add_fusion.1), channel_id=1, source_target_pairs={{0,32},{32,0},{8,40},{40,8},{16,48},{48,16},{24,56},{56,24},{64,96... | collective-permute-start | bytes 2359304 | tf_op jit(solution)/shard_map/ppermute | solution.py:16
  183.9 1.8 copy.150
  186.3 1.3 fusion.3
  187.6 1.7 fusion.13
  189.3 32.6 %collective-permute-done.7 = f32[3,4,128,128]{3,2,1,0:T(8,128)S(1)} collective-permute-done((f32[3,4,128,128]{3,2,1,0:T(8,128)S(1)}, f32[3,4,128,128]{3,2,1,0:T(8,128)S(1)}, u32[]{:S(2)}, u32[]{:S(2)}) %collective-permute-start.7) | collective-permute-done | bytes 786464 | tf_op jit(solution)/shard_map/ppermute | solution.py:16
  222.5 0.7 fusion.11
  223.2 0.7 fusion.9
  223.8 11.3 %collective-permute-done.8 = f32[2,4,128,128]{3,2,1,0:T(8,128)S(1)} collective-permute-done((f32[2,4,128,128]{3,2,1,0:T(8,128)S(1)}, f32[2,4,128,128]{3,2,1,0:T(8,128)S(1)}, u32[]{:S(2)}, u32[]{:S(2)}) %collective-permute-start.8) | collective-permute-done | bytes 524320 | tf_op jit(solution)/shard_map/ppermute | solution.py:16
  235.1 3.6 collective-permute-start.9
  238.7 0.7 fusion.7
  239.8 1.6 convert_bitcast_fusion.1
  241.4 1.9 collective-permute-done.9
  244.1 0.9 copy.152
  244.9 0.7 fusion.5
  245.6 0.9 copy.151
  246.5 117.7 %reduce-scatter.7.cloned.1.call-done = bf16[128,512]{1,0:T(8,128)(2,1)} async-done(((bf16[4096,512]{1,0:T(8,128)(2,1)}), bf16[128,512]{1,0:T(8,128)(2,1)}) %reduce-scatter.7.cloned.1.call-update) | async-done | bytes 131088
  364.2 1.0 copy.177
  365.2 0.7 convert_bitcast_fusion
  (74 shorter events, 11.2 us)
Async XLA Ops:
  7.2 1.0 copy-start
  7.2 31.8 %copy-start.3 = (f32[128,4,128]{2,1,0:T(4,128)S(1)}, f32[128,4,128]{2,1,0:T(4,128)}, u32[]{:S(2)}) copy-start(f32[128,4,128]{2,1,0:T(4,128)} %param.7) | copy-start | bytes 786436
  7.2 31.8 %copy-start.2 = (f32[128,4,128]{2,1,0:T(4,128)S(1)}, f32[128,4,128]{2,1,0:T(4,128)}, u32[]{:S(2)}) copy-start(f32[128,4,128]{2,1,0:T(4,128)} %param.6) | copy-start | bytes 786436
  7.2 65.2 %all-gather.2.cloned.1.call-start = ((), (), s32[]{:S(2)}) async-start(), calls=%async_computation.3 | async-start | bytes 1179648 | tf_op jit(solution)/shard_map/all_gather | solution.py:24
  9.7 8.3 %collective-permute-start = (f32[4,128,128]{2,1,0:T(8,128)S(1)}, f32[4,128,128]{2,1,0:T(8,128)S(1)}, u32[]{:S(2)}, u32[]{:S(2)}) collective-permute-start(f32[4,128,128]{2,1,0:T(8,128)S(1)} %fusion.60), channel_id=1, source_target_pairs={{0,8},{8,0},{16,24},{24,16},{32,40},{40,32},{48,56},{56,48},{64,72... | collective-permute-start | bytes 786440 | tf_op jit(solution)/shard_map/ppermute | solution.py:16
  11.7 228.1 %reduce-scatter.5.cloned.1.call-start = ((), (), s32[]{:S(2)}) async-start(), calls=%async_computation.2 | async-start | bytes 2359296 | tf_op jit(solution)/shard_map/reduce_scatter | solution.py:90
  18.0 14.6 %collective-permute-start.1 = (f32[4,128,128]{2,1,0:T(8,128)S(1)}, f32[4,128,128]{2,1,0:T(8,128)S(1)}, u32[]{:S(2)}, u32[]{:S(2)}) collective-permute-start(f32[4,128,128]{2,1,0:T(8,128)S(1)} %add.107), channel_id=1, source_target_pairs={{0,16},{16,0},{8,24},{24,8},{32,48},{48,32},{40,56},{56,40},{64,80... | collective-permute-start | bytes 786440 | tf_op jit(solution)/shard_map/ppermute | solution.py:16
  32.7 18.6 %copy-start.15 = (f32[7,4,128]{2,1,0:T(4,128)S(1)}, f32[7,4,128]{2,1,0:T(4,128)}, u32[]{:S(2)}) copy-start(f32[7,4,128]{2,1,0:T(4,128)} %param.9) | copy-start | bytes 43012
  32.7 18.0 %collective-permute-start.2 = (f32[4,128,128]{2,1,0:T(8,128)S(1)}, f32[4,128,128]{2,1,0:T(8,128)S(1)}, u32[]{:S(2)}, u32[]{:S(2)}) collective-permute-start(f32[4,128,128]{2,1,0:T(8,128)S(1)} %add.109), channel_id=1, source_target_pairs={{0,32},{32,0},{8,40},{40,8},{16,48},{48,16},{24,56},{56,24},{64,96... | collective-permute-start | bytes 786440 | tf_op jit(solution)/shard_map/ppermute | solution.py:16
  50.7 7.0 %collective-permute-start.3 = (f32[4,128,128]{2,1,0:T(8,128)S(1)}, f32[4,128,128]{2,1,0:T(8,128)S(1)}, u32[]{:S(2)}, u32[]{:S(2)}) collective-permute-start(f32[4,128,128]{2,1,0:T(8,128)S(1)} %add.111), channel_id=1, source_target_pairs={{0,64},{64,0},{8,72},{72,8},{16,80},{80,16},{24,88},{88,24},{32,96... | collective-permute-start | bytes 786440 | tf_op jit(solution)/shard_map/ppermute | solution.py:16
  57.8 10.0 %copy-start.1 = (bf16[512,4096]{1,0:T(8,128)(2,1)S(1)}, bf16[512,4096]{1,0:T(8,128)(2,1)}, u32[]{:S(2)}) copy-start(bf16[512,4096]{1,0:T(8,128)(2,1)} %param.10) | copy-start | bytes 12582916
  57.8 8.6 %collective-permute-start.4 = (f32[4,128,128]{2,1,0:T(8,128)S(1)}, f32[4,128,128]{2,1,0:T(8,128)S(1)}, u32[]{:S(2)}, u32[]{:S(2)}) collective-permute-start(f32[4,128,128]{2,1,0:T(8,128)S(1)} %add.113), channel_id=1, source_target_pairs={{0,128},{128,0},{8,136},{136,8},{16,144},{144,16},{24,152},{152,24... | collective-permute-start | bytes 786440 | tf_op jit(solution)/shard_map/ppermute | solution.py:16
  66.4 0.7 copy-start.7
  69.9 294.2 %reduce-scatter.7.cloned.1.call-start = ((), (), s32[]{:S(2)}) async-start(), calls=%async_computation.4 | async-start | bytes 4325376
  83.4 1.2 copy-start.4
  84.6 3.6 copy-start.10
  84.6 4.9 %copy-start.14 = (f32[128,4,128]{2,1,0:T(4,128)S(1)}, f32[128,4,128]{2,1,0:T(4,128)}, u32[]{:S(2)}) copy-start(f32[128,4,128]{2,1,0:T(4,128)} %get-tuple-element.17) | copy-start | bytes 786436
  88.1 2.6 copy-start.13
  88.2 3.9 %copy-start.12 = (f32[128,4,128]{2,1,0:T(4,128)S(1)}, f32[128,4,128]{2,1,0:T(4,128)}, u32[]{:S(2)}) copy-start(f32[128,4,128]{2,1,0:T(4,128)} %get-tuple-element.19) | copy-start | bytes 786436
  90.8 2.6 copy-start.11
  94.8 25.3 %collective-permute-start.5 = (f32[5,4,128,128]{3,2,1,0:T(8,128)}, f32[5,4,128,128]{3,2,1,0:T(8,128)}, u32[]{:S(2)}, u32[]{:S(2)}) collective-permute-start(f32[5,4,128,128]{3,2,1,0:T(8,128)} %get-tuple-element.40), channel_id=1, source_target_pairs={{0,8},{8,0},{16,24},{24,16},{32,40},{40,32},{48,56},{56,48},{64,72... | collective-permute-start | bytes 3932168 | tf_op jit(solution)/shard_map/ppermute | solution.py:16
  94.8 25.3 %copy-start.9 = (f32[1,4,128,128]{3,2,1,0:T(8,128)S(1)}, f32[1,4,128,128]{3,2,1,0:T(8,128)}, u32[]{:S(2)}) copy-start(f32[1,4,128,128]{3,2,1,0:T(8,128)} %get-tuple-element.41) | copy-start | bytes 786436
  120.1 7.6 %copy-start.8 = (f32[4,128,128]{2,1,0:T(8,128)S(1)}, f32[4,128,128]{2,1,0:T(8,128)}, u32[]{:S(2)}) copy-start(f32[4,128,128]{2,1,0:T(8,128)} %copy-done.7) | copy-start | bytes 786436
  121.6 54.6 %collective-permute-start.6 = (f32[4,4,128,128]{3,2,1,0:T(8,128)S(1)}, f32[4,4,128,128]{3,2,1,0:T(8,128)S(1)}, u32[]{:S(2)}, u32[]{:S(2)}) collective-permute-start(f32[4,4,128,128]{3,2,1,0:T(8,128)S(1)} %slice_add_fusion), channel_id=1, source_target_pairs={{0,16},{16,0},{8,24},{24,8},{32,48},{48,32},{40,56},{56,40},{64,80... | collective-permute-start | bytes 3145736 | tf_op jit(solution)/shard_map/ppermute | solution.py:16
  176.2 1.0 copy-start.5
  177.2 44.8 %collective-permute-start.7 = (f32[3,4,128,128]{3,2,1,0:T(8,128)S(1)}, f32[3,4,128,128]{3,2,1,0:T(8,128)S(1)}, u32[]{:S(2)}, u32[]{:S(2)}) collective-permute-start(f32[3,4,128,128]{3,2,1,0:T(8,128)S(1)} %slice_add_fusion.1), channel_id=1, source_target_pairs={{0,32},{32,0},{8,40},{40,8},{16,48},{48,16},{24,56},{56,24},{64,96... | collective-permute-start | bytes 2359304 | tf_op jit(solution)/shard_map/ppermute | solution.py:16
  187.6 34.5 %copy-start.6 = (f32[4,4,128,128]{3,2,1,0:T(8,128)S(1)}, f32[4,4,128,128]{3,2,1,0:T(8,128)}, u32[]{:S(2)}) copy-start(f32[4,4,128,128]{3,2,1,0:T(8,128)} %copy-done.5) | copy-start | bytes 3145732
  222.0 13.1 %collective-permute-start.8 = (f32[2,4,128,128]{3,2,1,0:T(8,128)S(1)}, f32[2,4,128,128]{3,2,1,0:T(8,128)S(1)}, u32[]{:S(2)}, u32[]{:S(2)}) collective-permute-start(f32[2,4,128,128]{3,2,1,0:T(8,128)S(1)} %slice_add_fusion.2), channel_id=1, source_target_pairs={{0,64},{64,0},{8,72},{72,8},{16,80},{80,16},{24,88},{88,24},{32,96... | collective-permute-start | bytes 1572872 | tf_op jit(solution)/shard_map/ppermute | solution.py:16
  235.1 8.1 %collective-permute-start.9 = (f32[1,4,128,128]{3,2,1,0:T(8,128)S(1)}, f32[1,4,128,128]{3,2,1,0:T(8,128)S(1)}, u32[]{:S(2)}, u32[]{:S(2)}) collective-permute-start(f32[1,4,128,128]{3,2,1,0:T(8,128)S(1)} %slice_add_fusion.3), channel_id=1, source_target_pairs={{0,128},{128,0},{8,136},{136,8},{16,144},{144,16},{24,152},{152,24... | collective-permute-start | bytes 786440 | tf_op jit(solution)/shard_map/ppermute | solution.py:16
Sparse Core Ops, SparseCore 0:
  11.8 27.7 all-gather.1
  70.1 36.2 reduce-scatter.4
  110.2 253.8 reduce-scatter.6
where the time goes:
time: 374 us; the launch traced here: 372 us
  waiting for transfers between devices  270 us (72%)
  matrix products  34.9 us (9%)
  starting transfers between devices  32.1 us (9%)
  local copies, waits for them, and re-layouts  15.4 us (4%)
  between operations  14.1 us (4%)
  other arithmetic  5.84 us (2%)
    ppermute x10, waiting for transfers between devices, swapped(): return lax.ppermute(block, axis, route)  152 us
    unnamed x4, waiting for transfers between devices  118 us
    ppermute x10, starting transfers between devices, swapped(): return lax.ppermute(block, axis, route)  31.8 us
    unnamed x37, local copies, waits for them, and re-layouts  14.2 us
  transfers between devices with their start and end apart: 13, of which 11 were waited for; matrix products, arithmetic and copies ran while one was open for 13% of the time, Pallas kernels for 0%

commit v1 on v0

v1 whole, which is shorter than its diff:
```python
import functools

import jax
import jax.numpy as jnp
from jax import lax
from jax.experimental import pallas as pl
from jax.experimental.pallas import tpu as pltpu
from jax.sharding import PartitionSpec as P

MESH = pl.DeviceIdType.MESH
BF = jnp.bfloat16
F32 = jnp.float32
NN = (((1,), (0,)), ((), ()))
NT = (((1,), (1,)), ((), ()))
TN = (((0,), (0,)), ((), ()))
NY, NZ, NX = 4, 8, 4
HH = 4
HALF = 256


def mm(a, b, dims=NN):
    return lax.dot_general(a, b, dims, preferred_element_type=F32)


class Ids:
    def __init__(self):
        self.table = {}

    def __call__(self, *key):
        return self.table.setdefault(key, len(self.table))


def body_kernel(
    q_h, k_h, v_h, lam_h, wo_h, og_h,
    mixed_o, dq_o, dk_o, dv_o, pg_o,
    qf, kf, vf, lam_v, lam_s, lam_t, wo, gf, gacc,
    qb, kb, vb, gb, pb, db, attf, att16,
    sb, st, sty, tsend, trecv, s34, urecv, uacc,
    du, dd, ru, rd, dn,
    bb, at, cf, cu, cd, xu, xd,
    mp, mr, ms, mx,
    dqv, dkv, dvv, pgv, mixv,
    lsem, ssem, rsem,
):
    seq = lax.axis_index("seq")
    hd = lax.axis_index("head")
    y, z = lax.div(seq, NZ), lax.rem(seq, NZ)
    x, c = lax.div(hd, 2), lax.rem(hd, 2)
    sib = 1 - c

    def dev(yy, zz, xx, cc):
        return (yy * NZ + zz, xx * 2 + cc)

    def up(j):
        return lax.rem(z + j + NZ, NZ)

    def yp(j):
        return lax.rem(y + j + NY, NY)

    def xp(j):
        return lax.rem(x + j + NX, NX)

    d_sib = dev(y, z, x, sib)
    d_x = {j: dev(y, z, xp(j), c) for j in (1, 2, 3)}
    d_y = {j: dev(yp(j), z, x, c) for j in (1, 2, 3)}
    d_up, d_dn = dev(y, up(1), x, c), dev(y, up(-1), x, c)

    ids = Ids()
    pending = []

    def rcopy(src, dst, i, device):
        return pltpu.make_async_remote_copy(
            src_ref=src, dst_ref=dst, send_sem=ssem.at[i], recv_sem=rsem.at[i],
            device_id=device, device_id_type=MESH,
        )

    def send(src, dst, key, device):
        op = rcopy(src, dst, ids(*key), device)
        op.start()
        pending.append(op)

    def recv(dst, key, device):
        rcopy(dst, dst, ids(*key), device).wait_recv()

    loads = {}

    def load(name, src, dst):
        op = pltpu.make_async_copy(src, dst, lsem.at[len(loads)])
        op.start()
        loads[name] = op

    load("k", k_h, kf)
    load("v", v_h, vf)
    load("og", og_h, gf.at[hd])
    load("q", q_h, qf)
    load("lam", lam_h, lam_v)
    load("wo", wo_h, wo)

    barrier = pltpu.get_barrier_semaphore()
    partners = [d_sib] + [d_x[j] for j in (1, 2, 3)] + [d_y[j] for j in (1, 2, 3)] + [d_up, d_dn]
    for who in partners:
        pl.semaphore_signal(barrier, inc=1, device_id=who, device_id_type=MESH)
    pl.semaphore_wait(barrier, len(partners))

    for j in (2, 1, 3):
        send(og_h, gf.at[hd], ("og", j), d_x[j])
    send(og_h, gf.at[hd], ("og", 0), d_sib)

    loads["k"].wait()
    loads["v"].wait()

    def rows(ref, h):
        return ref[pl.ds(h, 128, stride=HH), :]

    for h in range(HH):
        kh = rows(kf, h).astype(BF)
        vh = rows(vf, h).astype(BF)
        kb[h] = kh
        vb[h] = vh
        sb[z, pl.ds(128 * h, 128), :] = mm(kh, vh, TN).astype(BF)

    def half(i):
        return pl.ds(HALF * i, HALF)

    def ag_send(k):
        su, sd = up(-k), up(k)
        for i in (0, 1):
            if k < 3 or i == 0:
                send(sb.at[su, half(i)], sb.at[su, half(i)], ("agu", k, i), d_up)
            if k < 3 or i == 1:
                send(sb.at[sd, half(i)], sb.at[sd, half(i)], ("agd", k, i), d_dn)

    def ag_recv(k, i, dirs=("u", "d")):
        if "u" in dirs:
            recv(sb.at[up(-k - 1), half(i)], ("agu", k, i), d_up)
        if "d" in dirs:
            recv(sb.at[up(k + 1), half(i)], ("agd", k, i), d_dn)

    def ag_relay(k):
        su, sd = up(-k), up(k)
        for i in (0, 1):
            ag_recv(k - 1, i)
            if k < 3 or i == 0:
                send(sb.at[su, half(i)], sb.at[su, half(i)], ("agu", k, i), d_up)
            if k < 3 or i == 1:
                send(sb.at[sd, half(i)], sb.at[sd, half(i)], ("agd", k, i), d_dn)

    ag_send(0)

    loads["q"].wait()
    loads["lam"].wait()
    lam_s[...] = jnp.zeros_like(lam_s)
    for l in range(7):
        lam_s[pl.ds(4 * l, 4), :] = lam_v[l]
    lam_t[...] = lam_s[...].T

    def lam(l, h):
        return lam_t[:, 4 * l + h : 4 * l + h + 1]

    t_pos = lax.broadcasted_iota(jnp.int32, (128, 128), 0)
    s_pos = lax.broadcasted_iota(jnp.int32, (128, 128), 1)
    causal = t_pos >= s_pos
    cross = (t_pos >= 64) & (s_pos < 64)

    def weight(h):
        return jnp.where(causal, jnp.where(cross, lam(1, h), lam(0, h)), 0.0)

    for h in range(HH):
        qh = rows(qf, h).astype(BF)
        qb[h] = qh
        probs = (mm(qh, kb[h], NT) * weight(h)).astype(BF)
        pb[h] = probs
        attf[h] = mm(probs, vb[h])

    ag_relay(1)

    loads["og"].wait()
    loads["wo"].wait()

    def g_part(index):
        cols = pl.ds(pl.multiple_of(index * 512, 512), 512)
        return mm(gf[index], wo[:, cols], NT)

    gacc[...] = g_part(hd)
    for j in (1, 3, 2):
        src = xp(-j) * 2 + c
        recv(gf.at[src], ("og", j), d_x[j])
        send(gf.at[src], gf.at[src], ("og2", j), d_sib)
    for j in (1, 2, 3):
        send(gf.at[yp(j) * 2 + c], bb.at[y, c], ("b", j), d_y[j])
    ag_relay(2)
    for j in (1, 3, 2):
        gacc[...] += g_part(xp(-j) * 2 + c)
    recv(gf.at[x * 2 + sib], ("og", 0), d_sib)
    gacc[...] += g_part(x * 2 + sib)
    for j in (1, 3, 2):
        src = xp(-j) * 2 + sib
        recv(gf.at[src], ("og2", j), d_sib)
        gacc[...] += g_part(src)
    for h in range(HH):
        gb[h] = gacc[:, 128 * h : 128 * h + 128].astype(BF)
    for i in (0, 1):
        bb[y, i] = gf[y * 2 + i]

    ag_relay(3)

    def weighted(h, level):
        return (qb[h].astype(F32) * lam(level, h)).astype(BF)

    for d in (4, 3):
        for h in range(HH):
            sty[d - 3, pl.ds(128 * h, 128), :] = mm(weighted(h, 2 + d), gb[h], TN).astype(BF)
    near = lax.rem(y, 2)
    for j in (1, 2, 3):

        @pl.when(y >= j)
        def _(j=j):
            which = 1 - near if j == 1 else 1
            rcopy(sty.at[which], urecv.at[j - 1], ids("u", j), d_y[4 - j]).start()

    for d in (0, 1, 2):
        for h in range(HH):
            st[d, pl.ds(128 * h, 128), :] = mm(weighted(h, 2 + d), gb[h], TN)

    for h in range(HH):
        db[h] = (mm(gb[h], vb[h], NT) * weight(h)).astype(BF)
        dqv[pl.ds(h, 128, stride=HH), :] = mm(db[h], kb[h])
        dkv[pl.ds(h, 128, stride=HH), :] = mm(db[h], qb[h], TN)
        dvv[pl.ds(h, 128, stride=HH), :] = mm(pb[h], gb[h], TN)

    ag_recv(3, 0, "u")
    ag_recv(3, 1, "d")
    z1 = z + 1 - 2 * lax.rem(z, 2)
    zp = lax.div(z, 2)
    zp1 = 2 * (zp + 1 - 2 * lax.rem(zp, 2))
    zq1 = 4 * (1 - lax.div(z, 4))
    total = sb[0].astype(F32)
    for i in range(1, NZ):
        total = total + sb[i].astype(F32)
    tsend[...] = total.astype(BF)
    for j in (1, 2, 3):

        @pl.when(y + j < NY)
        def _(j=j):
            rcopy(tsend, trecv.at[j - 1], ids("t", j), d_y[j]).start()

    pair = (sb[zp1].astype(F32) + sb[zp1 + 1].astype(F32)).astype(BF)
    quad = sb[zq1].astype(F32)
    for i in range(1, 4):
        quad = quad + sb[zq1 + i].astype(F32)
    quad = quad.astype(BF)
    single = sb[z1]
    b0 = lax.rem(z, 2).astype(F32)
    b1 = lax.rem(zp, 2).astype(F32)
    b2 = lax.div(z, 4).astype(F32)

    def from_states(states, levels, bits):
        for h in range(HH):
            block = jnp.concatenate([s[128 * h : 128 * h + 128] for s in states], axis=0)
            wide = jnp.concatenate([s[128 * h : 128 * h + 128] for s in states], axis=1)
            qw, gw = [], []
            for l, bit in zip(levels, bits):
                scale = lam(l, h) if bit is None else lam(l, h) * bit
                qw.append((qb[h].astype(F32) * scale).astype(BF))
                gw.append((gb[h].astype(F32) * scale).astype(BF))
            attf[h] += mm(jnp.concatenate(qw, axis=1), block)
            place = pl.ds(h, 128, stride=HH)
            dqv[place, :] = dqv[place, :] + mm(jnp.concatenate(gw, axis=1), wide, NT)

    from_states([single, pair, quad], (2, 3, 4), (b0, b1, b2))

    def rs_step(k, own, bu, bd, pu, pd, tag):
        tu, td = up(4 - k), up(k - 4)
        for i in (0, 1):
            if k > 0 or i == 0:
                value = own(tu, i)
                if k > 1 or (k == 1 and i == 0):
                    recv(pu.at[k - 1, half(i)], (tag, "u", k - 1, i), d_up)
                    value = value + pu[k - 1, half(i), :].astype(F32)
                bu[k, half(i), :] = value.astype(BF)
                send(bu.at[k, half(i)], pu.at[k, half(i)], (tag, "u", k, i), d_up)
            if k > 0 or i == 1:
                value = own(td, i)
                if k > 1 or (k == 1 and i == 1):
                    recv(pd.at[k - 1, half(i)], (tag, "d", k - 1, i), d_dn)
                    value = value + pd[k - 1, half(i), :].astype(F32)
                bd[k, half(i), :] = value.astype(BF)
                send(bd.at[k, half(i)], pd.at[k, half(i)], (tag, "d", k, i), d_dn)

    def rs_final(i, own, pu, pd, tag):
        recv(pu.at[3, half(i)], (tag, "u", 3, i), d_up)
        recv(pd.at[3, half(i)], (tag, "d", 3, i), d_dn)
        return own(z, i) + pu[3, half(i), :].astype(F32) + pd[3, half(i), :].astype(F32)

    uacc[...] = jnp.zeros_like(uacc)
    for j in (1, 2, 3):

        @pl.when(y + j < NY)
        def _(j=j):
            recv(urecv.at[j - 1], ("u", j), d_y[4 - j])
            uacc[...] += urecv[j - 1].astype(F32)

    def own_d(zd, i):
        far = lax.div(z, 4) != lax.div(zd, 4)
        mid = lax.div(z, 2) != lax.div(zd, 2)
        level = jnp.where(far, 2, jnp.where(mid, 1, 0))
        on = (z > zd).astype(F32)
        return uacc[half(i), :] + on * st[level, half(i), :]

    rs_d = functools.partial(rs_step, own=own_d, bu=du, bd=dd, pu=ru, pd=rd, tag="d")
    rs_d(0)

    s34[...] = jnp.zeros_like(s34)
    for j in (1, 2, 3):

        @pl.when(y >= j)
        def _(j=j):
            which = 1 - near if j == 1 else 1
            recv(trecv.at[j - 1], ("t", j), d_y[j])
            s34[which] = s34[which] + trecv[j - 1].astype(F32)

    from_states([s34[0].astype(BF), s34[1].astype(BF)], (5, 6), (None, None))
    for h in range(HH):
        a16 = attf[h].astype(BF)
        att16[:, 128 * h : 128 * h + 128] = a16
        at[y, pl.ds(128 * h, 128), :] = a16.T
    for j in (1, 2, 3):
        send(at.at[y], at.at[y], ("at", j), d_y[j])
    dq_copy = pltpu.make_async_copy(dqv, dq_o, lsem.at[len(loads)])
    dq_copy.start()
    rs_d(1)

    def m_part(index):
        cols = pl.ds(pl.multiple_of(index * 512, 512), 512)
        return mm(att16[...], wo[:, cols]).astype(BF)

    for i in range(NX):
        mp[0, i] = m_part(i * 2 + sib)
    send(mp.at[0], mr, ("m",), d_sib)
    rs_d(2)
    for i in range(NX):
        mp[1, i] = m_part(i * 2 + c)

    for j in (1, 2, 3):
        src = yp(-j)
        recv(bb.at[src, c], ("b", j), d_y[j])
        send(bb.at[src, c], bb.at[src, c], ("b2", j), d_sib)
    recv(mr, ("m",), d_sib)
    for j in (2, 1, 3):
        ms[j - 1] = (mp[1, xp(j)].astype(F32) + mr[xp(j)].astype(F32)).astype(BF)
        send(ms.at[j - 1], mx.at[j - 1], ("mx", j), d_x[j])
    rs_d(3)
    for j in (1, 2, 3):
        recv(bb.at[yp(-j), sib], ("b2", j), d_sib)
    for j in (1, 3, 2):
        recv(at.at[yp(-j)], ("at", j), d_y[j])

    def c_part(n):
        a = jnp.concatenate([at[i] for i in range(NY)], axis=1)
        b = jnp.concatenate(
            [bb[i, n // 2, :, 256 * (n % 2) : 256 * (n % 2) + 256] for i in range(NY)], axis=0
        )
        out = mm(a, b)
        cf[2 * n] = out[:, :128]
        cf[2 * n + 1] = out[:, 128:]

    for n in range(4):
        c_part(n)

    def own_c(zd, i):
        return cf[zd, half(i), :]

    rs_c = functools.partial(rs_step, own=own_c, bu=cu, bd=cd, pu=xu, pd=xd, tag="c")
    rs_c(0)
    rs_c(1)

    for i in (0, 1):
        dn[half(i), :] = rs_final(i, own_d, ru, rd, "d").astype(BF)
    for h in range(HH):
        place = pl.ds(h, 128, stride=HH)
        block = dn[pl.ds(128 * h, 128), :]
        dkv[place, :] = dkv[place, :] + mm(vb[h], block, NT)
        dvv[place, :] = dvv[place, :] + mm(kb[h], block)
    dk_copy = pltpu.make_async_copy(dkv, dk_o, lsem.at[len(loads) + 1])
    dk_copy.start()
    dv_copy = pltpu.make_async_copy(dvv, dv_o, lsem.at[len(loads) + 2])
    dv_copy.start()
    rs_c(2)

    out = mp[1, x].astype(F32) + mr[x].astype(F32)
    for j in (1, 3, 2):
        recv(mx.at[j - 1], ("mx", j), d_x[j])
        out = out + mx[j - 1].astype(F32)
    mixv[...] = out.astype(BF)
    mix_copy = pltpu.make_async_copy(mixv, mixed_o, lsem.at[len(loads) + 3])
    mix_copy.start()
    rs_c(3)
    for i in (0, 1):
        pgv[half(i), :] = rs_final(i, own_c, xu, xd, "c")
    pg_copy = pltpu.make_async_copy(pgv, pg_o, lsem.at[len(loads) + 4])
    pg_copy.start()

    for op in pending:
        op.wait_send()
    for j in (1, 2, 3):

        @pl.when(y >= j)
        def _(j=j):
            which = 1 - near if j == 1 else 1
            rcopy(sty.at[which], urecv.at[j - 1], ids("u", j), d_y[4 - j]).wait_send()

        @pl.when(y + j < NY)
        def _(j=j):
            rcopy(tsend, trecv.at[j - 1], ids("t", j), d_y[j]).wait_send()

    for op in (dq_copy, dk_copy, dv_copy, mix_copy, pg_copy):
        op.wait()
    assert len(ids.table) <= N_SEM, len(ids.table)


N_SEM = 72


def body(queries, keys, values, level_weights, out_proj, out_grad):
    def flat(a):
        return a.reshape(512, 128)

    any_spec = pl.BlockSpec(memory_space=pl.ANY)
    blk = (512, 128)
    v = pltpu.VMEM
    outs = pl.pallas_call(
        body_kernel,
        out_shape=(
            jax.ShapeDtypeStruct((128, 512), BF),
            jax.ShapeDtypeStruct(blk, F32),
            jax.ShapeDtypeStruct(blk, F32),
            jax.ShapeDtypeStruct(blk, F32),
            jax.ShapeDtypeStruct(blk, F32),
        ),
        in_specs=[any_spec] * 6,
        out_specs=[any_spec] * 5,
        scratch_shapes=[
            v(blk, F32), v(blk, F32), v(blk, F32),
            v((7, 4, 128), F32), v((32, 128), F32), v((128, 32), F32),
            v((512, 4096), BF), v((8, 128, 512), BF), v((128, 512), F32),
            v((4, 128, 128), BF), v((4, 128, 128), BF), v((4, 128, 128), BF), v((4, 128, 128), BF),
            v((4, 128, 128), BF), v((4, 128, 128), BF), v((4, 128, 128), F32), v((128, 512), BF),
            v((8, 512, 128), BF), v((3, 512, 128), F32), v((2, 512, 128), BF),
            v(blk, BF), v((3, 512, 128), BF), v((2, 512, 128), F32), v((3, 512, 128), BF), v(blk, F32),
            v((4, 512, 128), BF), v((4, 512, 128), BF), v((4, 512, 128), BF), v((4, 512, 128), BF), v(blk, BF),
            v((4, 2, 128, 512), BF), v((4, 512, 128), BF), v((8, 512, 128), F32),
            v((4, 512, 128), BF), v((4, 512, 128), BF), v((4, 512, 128), BF), v((4, 512, 128), BF),
            v((2, 4, 128, 512), BF), v((4, 128, 512), BF), v((3, 128, 512), BF), v((3, 128, 512), BF),
            v(blk, F32), v(blk, F32), v(blk, F32), v(blk, F32), v((128, 512), BF),
            pltpu.SemaphoreType.DMA((12,)),
            pltpu.SemaphoreType.DMA((N_SEM,)),
            pltpu.SemaphoreType.DMA((N_SEM,)),
        ],
        compiler_params=pltpu.CompilerParams(
            collective_id=0, has_side_effects=True, vmem_limit_bytes=56 << 20
        ),
        name="log_linear",
    )(flat(queries), flat(keys), flat(values), level_weights, out_proj, out_grad)
    mixed, dq, dk, dv, pg = outs
    heads = queries.shape
    return mixed, dq.reshape(heads), dk.reshape(heads), dv.reshape(heads), pg


def solution(mesh):
    placed = (
        P("seq", "head", None),
        P("seq", "head", None),
        P("seq", "head", None),
        P(None, "head", "seq"),
        P("head", None),
        P("seq", "head"),
    )
    return jax.shard_map(
        body,
        mesh=mesh,
        in_specs=placed,
        out_specs=(
            P("seq", "head"),
            P("seq", "head", None),
            P("seq", "head", None),
            P("seq", "head", None),
            P("head", "seq"),
        ),
        check_vma=False,
    )
```

time: 374 us -> 71.3 us (0.19)
  waiting for transfers between devices: 270 us -> 0 us
  Pallas kernels: 0 us -> 62.2 us
  matrix products: 34.9 us -> 0 us
  starting transfers between devices: 32.1 us -> 0 us
  between operations: 14.1 us -> 0.64 us
  local copies, waits for them, and re-layouts: 15.4 us -> 8.24 us
  other arithmetic: 5.84 us -> 0 us
    ppermute x10 -> x0, waiting for transfers between devices: 152 us -> none  [swapped(): return lax.ppermute(block, axis, route)]
    unnamed x4 -> x0, waiting for transfers between devices: 118 us -> none
    pallas_call x0 -> x1, Pallas kernels: none -> 62.2 us  [body(): pl.pallas_call(body_kernel, out_shape=(jax.ShapeDtypeStruct((128, 512), B...]
    dot_general x35 -> x0, matrix products: 34.9 us -> none  [the longest x5 6.6 us: body(): jnp.einsum('thd,the->hde', queries * weights_rows[1 + local_bits + digit]...]
    ppermute x10 -> x0, starting transfers between devices: 31.8 us -> none  [swapped(): return lax.ppermute(block, axis, route)]
    unnamed x37 -> x5, local copies, waits for them, and re-layouts: 14.2 us -> 8.24 us
  transfers between devices with their start and end apart: 13 -> 0, of which waited for: 11 -> 0; matrix products, arithmetic and copies ran while one was open for 13% -> 0% of each run, Pallas kernels for 0% -> 0%
where the time goes in v1:
time: 71.3 us; the launch traced here: 71.1 us
  Pallas kernels  62.2 us (87%)
  local copies, waits for them, and re-layouts  8.24 us (12%)
    pallas_call x1, Pallas kernels, body(): pl.pallas_call(body_kernel, out_shape=(jax.ShapeDtypeStruct((128, 512), B...  62.2 us
    unnamed x5, local copies, waits for them, and re-layouts  8.24 us

profile of v1, /device:TPU:8, one launch (start us, length us, event | category | flops | bytes accessed | tf_op | source)
XLA Modules:
  0.0 71.1 jit_solution(16484639108796307307)
XLA Ops:
  0.6 62.2 %log_linear.1 = (bf16[128,512]{1,0:T(8,128)(2,1)}, f32[512,128]{1,0:T(8,128)}, f32[512,128]{1,0:T(8,128)}, f32[512,128]{1,0:T(8,128)}, f32[512,128]{1,0:T(8,128)}) custom-call(f32[512,128]{1,0:T(8,128)} %bitcast.9, f32[512,128]{1,0:T(8,128)} %bitcast.10, f32[512,128]{1,0:T(8,128)} %bitcast.11, f32[7,4,128]{2,1,0:T(4,128)} %lam_h.1, bf16[512,4096]{1,0:T(8,128)(2,1)} %wo_h.1, ...), custom_call_target="tpu_custom_call" | custom-call | tf_op jit(solution)/shard_map/log_linear/pallas_call | solution.py:431
  62.8 1.6 %copy.16 = bf16[128,512]{1,0:T(8,128)(2,1)} copy(bf16[128,512]{1,0:T(8,128)(2,1)} %get-tuple-element.20) | data formatting | bytes 262144
  64.4 1.7 %copy.17 = f32[128,4,128]{2,1,0:T(4,128)} copy(f32[128,4,128]{2,1,0:T(4,128)} %bitcast.8) | data formatting | bytes 524288
  66.1 1.7 %copy.18 = f32[128,4,128]{2,1,0:T(4,128)} copy(f32[128,4,128]{2,1,0:T(4,128)} %bitcast.7) | data formatting | bytes 524288
  67.7 1.7 %copy.19 = f32[128,4,128]{2,1,0:T(4,128)} copy(f32[128,4,128]{2,1,0:T(4,128)} %bitcast.6) | data formatting | bytes 524288
  69.4 1.7 %copy.20 = f32[512,128]{1,0:T(8,128)} copy(f32[512,128]{1,0:T(8,128)} %get-tuple-element.24) | data formatting | bytes 524288

commit v2 on v1

v2 whole, which is shorter than its diff:
```python
import functools

import jax
import jax.numpy as jnp
from jax import lax
from jax.experimental import pallas as pl
from jax.experimental.pallas import tpu as pltpu
from jax.sharding import PartitionSpec as P

MESH = pl.DeviceIdType.MESH
BF = jnp.bfloat16
F32 = jnp.float32
NN = (((1,), (0,)), ((), ()))
NT = (((1,), (1,)), ((), ()))
TN = (((0,), (0,)), ((), ()))
NY, NZ, NX = 4, 8, 4
HH = 4
HALF = 256


def mm(a, b, dims=NN):
    return lax.dot_general(a, b, dims, preferred_element_type=F32)


class Ids:
    def __init__(self):
        self.table = {}

    def __call__(self, *key):
        return self.table.setdefault(key, len(self.table))


def body_kernel(
    q_h, k_h, v_h, lam_h, wo_h, og_h,
    mixed_o, dq_o, dk_o, dv_o, pg_o,
    qf, kf, vf, lam_v, lam_s, lam_t, wo, gf, gacc,
    qb, kb, vb, gb, pb, db, attf, att16,
    sb, st, sty, tsend, trecv, s34, urecv, uacc,
    du, dd, ru, rd, dn,
    bb, at, cf, cu, cd, xu, xd,
    mp, mr, ms, mx,
    lsem, ssem, rsem,
):
    seq = lax.axis_index("seq")
    hd = lax.axis_index("head")
    y, z = lax.div(seq, NZ), lax.rem(seq, NZ)
    x, c = lax.div(hd, 2), lax.rem(hd, 2)
    sib = 1 - c

    def dev(yy, zz, xx, cc):
        return (yy * NZ + zz, xx * 2 + cc)

    def up(j):
        return lax.rem(z + j + NZ, NZ)

    def yp(j):
        return lax.rem(y + j + NY, NY)

    def xp(j):
        return lax.rem(x + j + NX, NX)

    d_sib = dev(y, z, x, sib)
    d_x = {j: dev(y, z, xp(j), c) for j in (1, 2, 3)}
    d_y = {j: dev(yp(j), z, x, c) for j in (1, 2, 3)}
    d_up, d_dn = dev(y, up(1), x, c), dev(y, up(-1), x, c)

    ids = Ids()
    pending = []

    def rcopy(src, dst, i, device):
        return pltpu.make_async_remote_copy(
            src_ref=src, dst_ref=dst, send_sem=ssem.at[i], recv_sem=rsem.at[i],
            device_id=device, device_id_type=MESH,
        )

    def send(src, dst, key, device):
        op = rcopy(src, dst, ids(*key), device)
        op.start()
        pending.append(op)

    def recv(dst, key, device):
        rcopy(dst, dst, ids(*key), device).wait_recv()

    loads = {}

    def load(name, src, dst):
        op = pltpu.make_async_copy(src, dst, lsem.at[len(loads)])
        op.start()
        loads[name] = op

    load("k", k_h, kf)
    load("v", v_h, vf)
    load("og", og_h, gf.at[hd])
    load("q", q_h, qf)
    load("lam", lam_h, lam_v)
    load("wo", wo_h, wo)

    barrier = pltpu.get_barrier_semaphore()
    partners = [d_sib] + [d_x[j] for j in (1, 2, 3)] + [d_y[j] for j in (1, 2, 3)] + [d_up, d_dn]
    for who in partners:
        pl.semaphore_signal(barrier, inc=1, device_id=who, device_id_type=MESH)

    def head(h):
        return pl.ds(128 * h, 128)

    def rows(ref, h):
        return ref[pl.ds(h, 128, stride=HH), :]

    loads["k"].wait()
    loads["v"].wait()
    for h in range(HH):
        kh = rows(kf, h).astype(BF)
        vh = rows(vf, h).astype(BF)
        kb[h] = kh
        vb[h] = vh
        sb[z, head(h), :] = mm(kh, vh, TN).astype(BF)

    pl.semaphore_wait(barrier, len(partners))

    for j in (1, 3, 2):
        send(og_h, gf.at[hd], ("og", j), d_x[j])

    def ag_send(k, h):
        su, sd = up(-k), up(k)
        if k < 3 or h < 2:
            send(sb.at[su, head(h)], sb.at[su, head(h)], ("agu", k, h), d_up)
        if k < 3 or h >= 2:
            send(sb.at[sd, head(h)], sb.at[sd, head(h)], ("agd", k, h), d_dn)

    def ag_recv(k, h):
        if k < 3 or h < 2:
            recv(sb.at[up(-k - 1), head(h)], ("agu", k, h), d_up)
        if k < 3 or h >= 2:
            recv(sb.at[up(k + 1), head(h)], ("agd", k, h), d_dn)

    def ag_relay(k, heads=range(HH)):
        for h in heads:
            ag_recv(k - 1, h)
            ag_send(k, h)

    for h in range(HH):
        ag_send(0, h)
    send(og_h, gf.at[hd], ("og", 0), d_sib)

    loads["q"].wait()
    loads["lam"].wait()
    lam_s[...] = jnp.zeros_like(lam_s)
    for l in range(7):
        lam_s[pl.ds(4 * l, 4), :] = lam_v[l]
    lam_t[...] = lam_s[...].T

    def lam(l, h):
        return lam_t[:, 4 * l + h : 4 * l + h + 1]

    t_pos = lax.broadcasted_iota(jnp.int32, (128, 128), 0)
    s_pos = lax.broadcasted_iota(jnp.int32, (128, 128), 1)
    causal = t_pos >= s_pos
    cross = (t_pos >= 64) & (s_pos < 64)

    def weight(h):
        return jnp.where(causal, jnp.where(cross, lam(1, h), lam(0, h)), 0.0)

    for h in range(HH):
        qh = rows(qf, h).astype(BF)
        qb[h] = qh
        probs = (mm(qh, kb[h], NT) * weight(h)).astype(BF)
        pb[h] = probs
        attf[h] = mm(probs, vb[h])

    ag_relay(1)

    loads["og"].wait()
    loads["wo"].wait()

    def g_part(index):
        cols = pl.ds(pl.multiple_of(index * 512, 512), 512)
        return mm(gf[index], wo[:, cols], NT)

    gacc[...] = g_part(hd)
    recv(gf.at[x * 2 + sib], ("og", 0), d_sib)
    gacc[...] += g_part(x * 2 + sib)
    ag_relay(2, (0, 1))
    for j in (1, 3, 2):
        src = xp(-j) * 2 + c
        recv(gf.at[src], ("og", j), d_x[j])
        send(gf.at[src], gf.at[src], ("og2", j), d_sib)
    for j in (1, 2, 3):
        send(gf.at[yp(j) * 2 + c], bb.at[y, c], ("b", j), d_y[j])
    ag_relay(2, (2, 3))
    for j in (1, 3, 2):
        gacc[...] += g_part(xp(-j) * 2 + c)
    for j in (1, 3, 2):
        src = xp(-j) * 2 + sib
        recv(gf.at[src], ("og2", j), d_sib)
        gacc[...] += g_part(src)
    for h in range(HH):
        gb[h] = gacc[:, 128 * h : 128 * h + 128].astype(BF)

    def weighted(h, level):
        return (qb[h].astype(F32) * lam(level, h)).astype(BF)

    for d in (4, 3):
        for h in range(HH):
            sty[d - 3, head(h), :] = mm(weighted(h, 2 + d), gb[h], TN).astype(BF)
    near = lax.rem(y, 2)
    for j in (1, 2, 3):

        @pl.when(y >= j)
        def _(j=j):
            which = 1 - near if j == 1 else 1
            rcopy(sty.at[which], urecv.at[j - 1], ids("u", j), d_y[4 - j]).start()

    ag_relay(3)
    for i in (0, 1):
        bb[y, i] = gf[y * 2 + i]
    for d in (0, 1, 2):
        for h in range(HH):
            st[d, head(h), :] = mm(weighted(h, 2 + d), gb[h], TN)

    for i in (0, 1):
        for h in (2 * i, 2 * i + 1):
            ag_recv(3, h)
            total = sb[0, head(h), :].astype(F32)
            for n in range(1, NZ):
                total = total + sb[n, head(h), :].astype(F32)
            tsend[head(h), :] = total.astype(BF)
        part = pl.ds(HALF * i, HALF)
        for j in (1, 2, 3):

            @pl.when(y + j < NY)
            def _(j=j):
                rcopy(tsend.at[part], trecv.at[j - 1, part], ids("t", j, i), d_y[j]).start()

    def local_grads():
        for h in range(HH):
            db[h] = (mm(gb[h], vb[h], NT) * weight(h)).astype(BF)
            dq_o[pl.ds(h, 128, stride=HH), :] = mm(db[h], kb[h])
            dk_o[pl.ds(h, 128, stride=HH), :] = mm(db[h], qb[h], TN)
            dv_o[pl.ds(h, 128, stride=HH), :] = mm(pb[h], gb[h], TN)

    local_grads()

    z1 = z + 1 - 2 * lax.rem(z, 2)
    zp = lax.div(z, 2)
    zp1 = 2 * (zp + 1 - 2 * lax.rem(zp, 2))
    zq1 = 4 * (1 - lax.div(z, 4))
    b0 = lax.rem(z, 2).astype(F32)
    b1 = lax.rem(zp, 2).astype(F32)
    b2 = lax.div(z, 4).astype(F32)

    def from_states(h, states, levels, bits):
        block = jnp.concatenate(states, axis=0)
        wide = jnp.concatenate(states, axis=1)
        qw, gw = [], []
        for l, bit in zip(levels, bits):
            scale = lam(l, h) if bit is None else lam(l, h) * bit
            qw.append((qb[h].astype(F32) * scale).astype(BF))
            gw.append((gb[h].astype(F32) * scale).astype(BF))
        attf[h] += mm(jnp.concatenate(qw, axis=1), block)
        place = pl.ds(h, 128, stride=HH)
        dq_o[place, :] = dq_o[place, :] + mm(jnp.concatenate(gw, axis=1), wide, NT)

    for h in range(HH):
        pair = (sb[zp1, head(h), :].astype(F32) + sb[zp1 + 1, head(h), :].astype(F32)).astype(BF)
        quad = sb[zq1, head(h), :].astype(F32)
        for i in range(1, 4):
            quad = quad + sb[zq1 + i, head(h), :].astype(F32)
        from_states(h, [sb[z1, head(h), :], pair, quad.astype(BF)], (2, 3, 4), (b0, b1, b2))

    class Scatter:
        def __init__(self, tag, own, bu, bd, pu, pd):
            self.tag, self.own = tag, own
            self.side = {"u": (bu, pu, d_up), "d": (bd, pd, d_dn)}

        def step(self, k, h, way):
            first = (h < 2) == (way == "u")
            assert k > 0 or first
            buf, got, device = self.side[way]
            value = self.own(up(4 - k) if way == "u" else up(k - 4), h)
            if k > 1 or (k == 1 and first):
                recv(got.at[k - 1, head(h)], (self.tag, way, k - 1, h), device)
                value = value + got[k - 1, head(h), :].astype(F32)
            buf[k, head(h), :] = value.astype(BF)
            send(buf.at[k, head(h)], got.at[k, head(h)], (self.tag, way, k, h), device)

        def start(self, i):
            for h in (2 * i, 2 * i + 1):
                self.step(0, h, "ud"[i])
            for h in (2 * i, 2 * i + 1):
                self.step(1, h, "du"[i])

        def wave(self, k, pairs=((2, 0), (3, 1), (0, 2), (1, 3))):
            for a, b in pairs:
                self.step(k, a, "u")
                self.step(k, b, "d")

        def wave1(self):
            self.step(1, 0, "u")
            self.step(1, 2, "d")
            self.step(1, 1, "u")
            self.step(1, 3, "d")

        def final(self, h):
            total = self.own(z, h)
            for way in ("u", "d"):
                _, got, device = self.side[way]
                recv(got.at[3, head(h)], (self.tag, way, 3, h), device)
                total = total + got[3, head(h), :].astype(F32)
            return total

    for j in (1, 3, 2):
        src = yp(-j)
        recv(bb.at[src, c], ("b", j), d_y[j])
        send(bb.at[src, c], bb.at[src, c], ("b2", j), d_sib)

    uacc[...] = jnp.zeros_like(uacc)
    for j in (1, 2, 3):

        @pl.when(y + j < NY)
        def _(j=j):
            recv(urecv.at[j - 1], ("u", j), d_y[4 - j])
            uacc[...] += urecv[j - 1].astype(F32)

    def own_d(zd, h):
        far = lax.div(z, 4) != lax.div(zd, 4)
        mid = lax.div(z, 2) != lax.div(zd, 2)
        level = jnp.where(far, 2, jnp.where(mid, 1, 0))
        on = (z > zd).astype(F32)
        return uacc[head(h), :] + on * st[level, head(h), :]

    rs_d = Scatter("d", own_d, du, dd, ru, rd)
    rs_d.start(0)
    rs_d.start(1)

    s34[...] = jnp.zeros_like(s34)
    for i in (0, 1):
        part = pl.ds(HALF * i, HALF)
        for j in (1, 2, 3):

            @pl.when(y >= j)
            def _(j=j):
                which = 1 - near if j == 1 else 1
                recv(trecv.at[j - 1, part], ("t", j, i), d_y[j])
                s34[which, part, :] = s34[which, part, :] + trecv[j - 1, part, :].astype(F32)

        for h in (2 * i, 2 * i + 1):
            from_states(
                h, [s34[0, head(h), :].astype(BF), s34[1, head(h), :].astype(BF)], (5, 6), (None, None)
            )
            a16 = attf[h].astype(BF)
            att16[:, 128 * h : 128 * h + 128] = a16
            at[y, head(h), :] = a16.T
        for j in (1, 3, 2):
            send(at.at[y, part], at.at[y, part], ("at", j, i), d_y[j])
        if i == 0:
            rs_d.wave1()

    def m_part(index):
        cols = pl.ds(pl.multiple_of(index * 512, 512), 512)
        return mm(att16[...], wo[:, cols]).astype(BF)

    for i in range(NX):
        mp[0, i] = m_part(i * 2 + sib)
    send(mp.at[0], mr, ("m",), d_sib)
    rs_d.wave(2)
    for i in range(NX):
        mp[1, i] = m_part(i * 2 + c)
    recv(mr, ("m",), d_sib)
    for j in (1, 3, 2):
        ms[j - 1] = (mp[1, xp(j)].astype(F32) + mr[xp(j)].astype(F32)).astype(BF)
        send(ms.at[j - 1], mx.at[j - 1], ("mx", j), d_x[j])

    for j in (1, 2, 3):
        recv(bb.at[yp(-j), sib], ("b2", j), d_sib)

    def own_c(zd, h):
        return cf[zd, head(h), :]

    rs_c = Scatter("c", own_c, cu, cd, xu, xd)
    for i in (0, 1):
        part = pl.ds(HALF * i, HALF)
        for j in (1, 3, 2):
            recv(at.at[yp(-j), part], ("at", j, i), d_y[j])
        a = jnp.concatenate([at[n, part, :] for n in range(NY)], axis=1)
        for n in range(4):
            b = jnp.concatenate(
                [bb[m, n // 2, :, 256 * (n % 2) : 256 * (n % 2) + 256] for m in range(NY)], axis=0
            )
            out = mm(a, b)
            cf[2 * n, part, :] = out[:, :128]
            cf[2 * n + 1, part, :] = out[:, 128:]
        rs_c.start(i)
    rs_d.wave(3)
    rs_c.wave1()

    for h in range(HH):
        dn[head(h), :] = rs_d.final(h).astype(BF)
    rs_c.wave(2)
    for h in range(HH):
        place = pl.ds(h, 128, stride=HH)
        block = dn[head(h), :]
        dk_o[place, :] = dk_o[place, :] + mm(vb[h], block, NT)
        dv_o[place, :] = dv_o[place, :] + mm(kb[h], block)

    out = mp[1, x].astype(F32) + mr[x].astype(F32)
    for j in (1, 3, 2):
        recv(mx.at[j - 1], ("mx", j), d_x[j])
        out = out + mx[j - 1].astype(F32)
    mixed_o[...] = out.astype(BF)
    rs_c.wave(3)
    for h in (2, 3, 0, 1):
        pg_o[head(h), :] = rs_c.final(h)

    for op in pending:
        op.wait_send()
    for j in (1, 2, 3):

        @pl.when(y >= j)
        def _(j=j):
            which = 1 - near if j == 1 else 1
            rcopy(sty.at[which], urecv.at[j - 1], ids("u", j), d_y[4 - j]).wait_send()

        @pl.when(y + j < NY)
        def _(j=j):
            for i in (0, 1):
                part = pl.ds(HALF * i, HALF)
                rcopy(tsend.at[part], trecv.at[j - 1, part], ids("t", j, i), d_y[j]).wait_send()

    assert len(ids.table) <= N_SEM, len(ids.table)


N_SEM = 120
VLIM = 28


def out_kernel(*refs):
    src, dst, via = refs[:5], refs[5:10], refs[10:15]
    isem, osem = refs[15:]
    ins = [pltpu.make_async_copy(a, b, isem.at[i]) for i, (a, b) in enumerate(zip(src, via))]
    outs = [pltpu.make_async_copy(a, b, osem.at[i]) for i, (a, b) in enumerate(zip(via, dst))]
    for op in ins:
        op.start()
    for a, b in zip(ins, outs):
        a.wait()
        b.start()
    for op in outs:
        op.wait()


def body(queries, keys, values, level_weights, out_proj, out_grad):
    def flat(a):
        return a.reshape(512, 128)

    any_spec = pl.BlockSpec(memory_space=pl.ANY)
    blk = (512, 128)
    v = pltpu.VMEM
    outs = pl.pallas_call(
        body_kernel,
        out_shape=(
            jax.ShapeDtypeStruct((128, 512), BF),
            jax.ShapeDtypeStruct(blk, F32),
            jax.ShapeDtypeStruct(blk, F32),
            jax.ShapeDtypeStruct(blk, F32),
            jax.ShapeDtypeStruct(blk, F32),
        ),
        in_specs=[pl.BlockSpec(memory_space=pltpu.HBM)] * 6,
        out_specs=[pl.BlockSpec(memory_space=pltpu.VMEM)] * 5,
        scratch_shapes=[
            v(blk, F32), v(blk, F32), v(blk, F32),
            v((7, 4, 128), F32), v((32, 128), F32), v((128, 32), F32),
            v((512, 4096), BF), v((8, 128, 512), BF), v((128, 512), F32),
            v((4, 128, 128), BF), v((4, 128, 128), BF), v((4, 128, 128), BF), v((4, 128, 128), BF),
            v((4, 128, 128), BF), v((4, 128, 128), BF), v((4, 128, 128), F32), v((128, 512), BF),
            v((8, 512, 128), BF), v((3, 512, 128), F32), v((2, 512, 128), BF),
            v(blk, BF), v((3, 512, 128), BF), v((2, 512, 128), F32), v((3, 512, 128), BF), v(blk, F32),
            v((4, 512, 128), BF), v((4, 512, 128), BF), v((4, 512, 128), BF), v((4, 512, 128), BF), v(blk, BF),
            v((4, 2, 128, 512), BF), v((4, 512, 128), BF), v((8, 512, 128), F32),
            v((4, 512, 128), BF), v((4, 512, 128), BF), v((4, 512, 128), BF), v((4, 512, 128), BF),
            v((2, 4, 128, 512), BF), v((4, 128, 512), BF), v((3, 128, 512), BF), v((3, 128, 512), BF),
            pltpu.SemaphoreType.DMA((12,)),
            pltpu.SemaphoreType.DMA((N_SEM,)),
            pltpu.SemaphoreType.DMA((N_SEM,)),
        ],
        compiler_params=pltpu.CompilerParams(
            collective_id=0, has_side_effects=True, vmem_limit_bytes=VLIM << 20
        ),
        name="log_linear",
    )(*[pltpu.with_memory_space_constraint(a, pltpu.HBM) for a in (flat(queries), flat(keys), flat(values), level_weights, out_proj, out_grad)])
    mixed, dq, dk, dv, pg = pl.pallas_call(
        out_kernel,
        out_shape=tuple(jax.ShapeDtypeStruct(o.shape, o.dtype) for o in outs),
        in_specs=[any_spec] * 5,
        out_specs=[any_spec] * 5,
        scratch_shapes=[v(o.shape, o.dtype) for o in outs]
        + [pltpu.SemaphoreType.DMA((5,)), pltpu.SemaphoreType.DMA((5,))],
        compiler_params=pltpu.CompilerParams(vmem_limit_bytes=4 << 20),
        name="results",
    )(*outs)
    heads = queries.shape
    return mixed, dq.reshape(heads), dk.reshape(heads), dv.reshape(heads), pg


def solution(mesh):
    placed = (
        P("seq", "head", None),
        P("seq", "head", None),
        P("seq", "head", None),
        P(None, "head", "seq"),
        P("head", None),
        P("seq", "head"),
    )
    return jax.shard_map(
        body,
        mesh=mesh,
        in_specs=placed,
        out_specs=(
            P("seq", "head"),
            P("seq", "head", None),
            P("seq", "head", None),
            P("seq", "head", None),
            P("head", "seq"),
        ),
        check_vma=False,
    )
```

time: 71.3 us -> 60.1 us (0.84); the launches traced: 71.1 us -> 59 us
  local copies, waits for them, and re-layouts: 8.24 us -> 0 us
  Pallas kernels: 62.2 us -> 58.4 us
    unnamed x5 -> x0, local copies, waits for them, and re-layouts: 8.24 us -> none
    pallas_call x1, Pallas kernels: 62.2 us -> 57 us  [body(): pl.pallas_call(body_kernel, out_shape=(jax.ShapeDtypeStruct((128, 512), B...]
    pallas_call x0 -> x1, Pallas kernels: none -> 1.34 us  [body(): pl.pallas_call(out_kernel, out_shape=tuple((jax.ShapeDtypeStruct(o.shape,...]
where the time goes in v2:
time: 60.1 us; the launch traced here: 59 us
  Pallas kernels  58.4 us (97%)
  between operations  0.64 us (1%)
    pallas_call x1, Pallas kernels, body(): pl.pallas_call(body_kernel, out_shape=(jax.ShapeDtypeStruct((128, 512), B...  57 us
    pallas_call x1, Pallas kernels, body(): pl.pallas_call(out_kernel, out_shape=tuple((jax.ShapeDtypeStruct(o.shape,...  1.34 us

profile of v2, /device:TPU:8, one launch (start us, length us, event | category | flops | bytes accessed | tf_op | source)
XLA Modules:
  0.0 59.0 jit_solution(7855644607661992874)
XLA Ops:
  0.6 57.0 %log_linear.1 = (bf16[128,512]{1,0:T(8,128)(2,1)S(1)}, f32[512,128]{1,0:T(8,128)S(1)}, f32[512,128]{1,0:T(8,128)S(1)}, f32[512,128]{1,0:T(8,128)S(1)}, f32[512,128]{1,0:T(8,128)S(1)}) custom-call(f32[512,128]{1,0:T(8,128)} %bitcast.6, f32[512,128]{1,0:T(8,128)} %bitcast.7, f32[512,128]{1,0:T(8,128)} %bitcast.8, f32[7,4,128]{2,1,0:T(4,128)} %lam_h.1, ...), custom_call_target="tpu_custom_call" | custom-call | tf_op jit(solution)/shard_map/log_linear/pallas_call | solution.py:457
  57.7 1.3 %results.1 = (bf16[128,512]{1,0:T(8,128)(2,1)}, f32[512,128]{1,0:T(8,128)}, f32[512,128]{1,0:T(8,128)}, f32[512,128]{1,0:T(8,128)}, f32[512,128]{1,0:T(8,128)}) custom-call(bf16[128,512]{1,0:T(8,128)(2,1)S(1)} %get-tuple-element.15.refs_0_, f32[512,128]{1,0:T(8,128)S(1)} %get-tuple-element.16.refs_1_, f32[512,128]{1,0:T(8,128)S(1)} %get-tuple-element.17.refs_2_, ...), custom_call_target="tpu_custom_call" | custom-call | tf_op jit(solution)/shard_map/results/pallas_call | solution.py:489

commit v3 on v2

--- a/solution.py
+++ b/solution.py
@@ -1,4 +1,5 @@
 import functools
+import math
 
 import jax
 import jax.numpy as jnp
@@ -35,7 +36,7 @@
     mixed_o, dq_o, dk_o, dv_o, pg_o,
     qf, kf, vf, lam_v, lam_s, lam_t, wo, gf, gacc,
     qb, kb, vb, gb, pb, db, attf, att16,
-    sb, st, sty, tsend, trecv, s34, urecv, uacc,
+    sb, st, sty, tsend, trecv, s34, uwr, us, ur, usum, uall,
     du, dd, ru, rd, dn,
     bb, at, cf, cu, cd, xu, xd,
     mp, mr, ms, mx,
@@ -64,22 +65,27 @@
     d_y = {j: dev(yp(j), z, x, c) for j in (1, 2, 3)}
     d_up, d_dn = dev(y, up(1), x, c), dev(y, up(-1), x, c)
 
-    ids = Ids()
-    pending = []
-
-    def rcopy(src, dst, i, device):
+    ids, sids = Ids(), Ids()
+    group = {}
+
+    def rcopy(src, dst, key, device):
         return pltpu.make_async_remote_copy(
-            src_ref=src, dst_ref=dst, send_sem=ssem.at[i], recv_sem=rsem.at[i],
+            src_ref=src, dst_ref=dst, send_sem=ssem.at[sids(key[0])], recv_sem=rsem.at[ids(*key)],
             device_id=device, device_id_type=MESH,
         )
 
     def send(src, dst, key, device):
-        op = rcopy(src, dst, ids(*key), device)
-        op.start()
-        pending.append(op)
+        rcopy(src, dst, key, device).start()
+        group[key[0]] = group.get(key[0], 0) + math.prod(src.shape)
+
+    def sent(ref, name):
+        pltpu.make_async_remote_copy(
+            src_ref=ref, dst_ref=ref, send_sem=ssem.at[sids(name)], recv_sem=rsem.at[0],
+            device_id=d_sib, device_id_type=MESH,
+        ).wait_send()
 
     def recv(dst, key, device):
-        rcopy(dst, dst, ids(*key), device).wait_recv()
+        rcopy(dst, dst, key, device).wait_recv()
 
     loads = {}
 
@@ -123,15 +129,15 @@
     def ag_send(k, h):
         su, sd = up(-k), up(k)
         if k < 3 or h < 2:
-            send(sb.at[su, head(h)], sb.at[su, head(h)], ("agu", k, h), d_up)
+            send(sb.at[su, head(h)], sb.at[su, head(h)], ("ag", "u", k, h), d_up)
         if k < 3 or h >= 2:
-            send(sb.at[sd, head(h)], sb.at[sd, head(h)], ("agd", k, h), d_dn)
+            send(sb.at[sd, head(h)], sb.at[sd, head(h)], ("ag", "d", k, h), d_dn)
 
     def ag_recv(k, h):
         if k < 3 or h < 2:
-            recv(sb.at[up(-k - 1), head(h)], ("agu", k, h), d_up)
+            recv(sb.at[up(-k - 1), head(h)], ("ag", "u", k, h), d_up)
         if k < 3 or h >= 2:
-            recv(sb.at[up(k + 1), head(h)], ("agd", k, h), d_dn)
+            recv(sb.at[up(k + 1), head(h)], ("ag", "d", k, h), d_dn)
 
     def ag_relay(k, heads=range(HH)):
         for h in heads:
@@ -176,19 +182,23 @@
         cols = pl.ds(pl.multiple_of(index * 512, 512), 512)
         return mm(gf[index], wo[:, cols], NT)
 
+    def og_relay(j):
+        src = xp(-j) * 2 + c
+        recv(gf.at[src], ("og", j), d_x[j])
+        send(gf.at[src], gf.at[src], ("og2", j), d_sib)
+
     gacc[...] = g_part(hd)
     recv(gf.at[x * 2 + sib], ("og", 0), d_sib)
     gacc[...] += g_part(x * 2 + sib)
+    og_relay(1)
+    og_relay(3)
     ag_relay(2, (0, 1))
-    for j in (1, 3, 2):
-        src = xp(-j) * 2 + c
-        recv(gf.at[src], ("og", j), d_x[j])
-        send(gf.at[src], gf.at[src], ("og2", j), d_sib)
+    og_relay(2)
     for j in (1, 2, 3):
-        send(gf.at[yp(j) * 2 + c], bb.at[y, c], ("b", j), d_y[j])
-    ag_relay(2, (2, 3))
+        send(gf.at[yp(j) * 2 + c], bb.at[j, c], ("b", j), d_y[j])
     for j in (1, 3, 2):
         gacc[...] += g_part(xp(-j) * 2 + c)
+    ag_relay(2, (2, 3))
     for j in (1, 3, 2):
         src = xp(-j) * 2 + sib
         recv(gf.at[src], ("og2", j), d_sib)
@@ -203,42 +213,108 @@
         for h in range(HH):
             sty[d - 3, head(h), :] = mm(weighted(h, 2 + d), gb[h], TN).astype(BF)
     near = lax.rem(y, 2)
-    for j in (1, 2, 3):
-
-        @pl.when(y >= j)
-        def _(j=j):
-            which = 1 - near if j == 1 else 1
-            rcopy(sty.at[which], urecv.at[j - 1], ids("u", j), d_y[4 - j]).start()
+    main = jnp.where(y == 1, 0, 1)
+
+    def piece(n):
+        return pl.ds(pl.multiple_of(64 * n, 64), 64)
+
+    def u_sum(level, tag):
+        for j in range(1, NZ):
+            to = up(j)
+            rcopy(sty.at[level, piece(to)], uwr.at[level, j - 1], (tag,), dev(y, to, x, c)).start()
+
+    def u_total(level, tag):
+        recv(uwr.at[level], (tag,), d_up)
+        total = sty[level, piece(z), :].astype(F32)
+        for j in range(1, NZ):
+            total = total + uwr[level, j - 1].astype(F32)
+        us[level] = total.astype(BF)
 
     ag_relay(3)
-    for i in (0, 1):
-        bb[y, i] = gf[y * 2 + i]
+
     for d in (0, 1, 2):
         for h in range(HH):
             st[d, head(h), :] = mm(weighted(h, 2 + d), gb[h], TN)
 
+    class Scatter:
+        def __init__(self, tag, own, bu, bd, pu, pd):
+            self.tag, self.own = tag, own
+            self.side = {"u": (bu, pu, d_up), "d": (bd, pd, d_dn)}
+
+        def step(self, k, h, way):
+            first = (h < 2) == (way == "u")
+            assert k > 0 or first
+            buf, got, device = self.side[way]
+            value = self.own(up(4 - k) if way == "u" else up(k - 4), h)
+            if k > 1 or (k == 1 and first):
+                recv(got.at[k - 1, head(h)], (self.tag, way, k - 1, h), device)
+                value = value + got[k - 1, head(h), :].astype(F32)
+            buf[k, head(h), :] = value.astype(BF)
+            send(buf.at[k, head(h)], got.at[k, head(h)], (self.tag, way, k, h), device)
+
+        def start(self, i):
+            for h in (2 * i, 2 * i + 1):
+                self.step(0, h, "ud"[i])
+            for h in (2 * i, 2 * i + 1):
+                self.step(1, h, "du"[i])
+
+        def wave(self, k, pairs=((2, 0), (3, 1), (0, 2), (1, 3))):
+            for a, b in pairs:
+                self.step(k, a, "u")
+                self.step(k, b, "d")
+
+        def wave1(self):
+            self.step(1, 0, "u")
+            self.step(1, 2, "d")
+            self.step(1, 1, "u")
+            self.step(1, 3, "d")
+
+        def final(self, h):
+            total = self.own(z, h)
+            for way in ("u", "d"):
+                _, got, device = self.side[way]
+                recv(got.at[3, head(h)], (self.tag, way, 3, h), device)
+                total = total + got[3, head(h), :].astype(F32)
+            return total
+
+    def own_d(zd, h):
+        far = lax.div(z, 4) != lax.div(zd, 4)
+        mid = lax.div(z, 2) != lax.div(zd, 2)
+        level = jnp.where(far, 2, jnp.where(mid, 1, 0))
+        on = (z > zd).astype(F32)
+        return on * st[level, head(h), :]
+
+    rs_d = Scatter("d", own_d, du, dd, ru, rd)
+    rs_d.start(0)
+    rs_d.start(1)
     for i in (0, 1):
-        for h in (2 * i, 2 * i + 1):
-            ag_recv(3, h)
-            total = sb[0, head(h), :].astype(F32)
-            for n in range(1, NZ):
-                total = total + sb[n, head(h), :].astype(F32)
-            tsend[head(h), :] = total.astype(BF)
-        part = pl.ds(HALF * i, HALF)
+        bb[0, i] = gf[y * 2 + i]
+
+    for h in range(HH):
+        ag_recv(3, h)
+        total = sb[0, head(h), :].astype(F32)
+        for n in range(1, NZ):
+            total = total + sb[n, head(h), :].astype(F32)
+        tsend[head(h), :] = total.astype(BF)
         for j in (1, 2, 3):
 
             @pl.when(y + j < NY)
             def _(j=j):
-                rcopy(tsend.at[part], trecv.at[j - 1, part], ids("t", j, i), d_y[j]).start()
-
-    def local_grads():
-        for h in range(HH):
-            db[h] = (mm(gb[h], vb[h], NT) * weight(h)).astype(BF)
-            dq_o[pl.ds(h, 128, stride=HH), :] = mm(db[h], kb[h])
-            dk_o[pl.ds(h, 128, stride=HH), :] = mm(db[h], qb[h], TN)
-            dv_o[pl.ds(h, 128, stride=HH), :] = mm(pb[h], gb[h], TN)
-
-    local_grads()
+                rcopy(tsend.at[head(h)], trecv.at[j - 1, head(h)], ("t%d" % j, h), d_y[j]).start()
+
+    @pl.when(y > 0)
+    def _():
+        u_sum(main, "u1")
+
+    @pl.when(y == 3)
+    def _():
+        u_sum(0, "u2")
+
+    for h in range(HH):
+        db[h] = (mm(gb[h], vb[h], NT) * weight(h)).astype(BF)
+        dq_o[pl.ds(h, 128, stride=HH), :] = mm(db[h], kb[h])
+        dk_o[pl.ds(h, 128, stride=HH), :] = mm(db[h], qb[h], TN)
+        dv_o[pl.ds(h, 128, stride=HH), :] = mm(pb[h], gb[h], TN)
 
     z1 = z + 1 - 2 * lax.rem(z, 2)
     zp = lax.div(z, 2)
@@ -267,93 +343,47 @@
             quad = quad + sb[zq1 + i, head(h), :].astype(F32)
         from_states(h, [sb[z1, head(h), :], pair, quad.astype(BF)], (2, 3, 4), (b0, b1, b2))
 
-    class Scatter:
-        def __init__(self, tag, own, bu, bd, pu, pd):
-            self.tag, self.own = tag, own
-            self.side = {"u": (bu, pu, d_up), "d": (bd, pd, d_dn)}
-
-        def step(self, k, h, way):
-            first = (h < 2) == (way == "u")
-            assert k > 0 or first
-            buf, got, device = self.side[way]
-            value = self.own(up(4 - k) if way == "u" else up(k - 4), h)
-            if k > 1 or (k == 1 and first):
-                recv(got.at[k - 1, head(h)], (self.tag, way, k - 1, h), device)
-                value = value + got[k - 1, head(h), :].astype(F32)
-            buf[k, head(h), :] = value.astype(BF)
-            send(buf.at[k, head(h)], got.at[k, head(h)], (self.tag, way, k, h), device)
-
-        def start(self, i):
-            for h in (2 * i, 2 * i + 1):
-                self.step(0, h, "ud"[i])
-            for h in (2 * i, 2 * i + 1):
-                self.step(1, h, "du"[i])
-
-        def wave(self, k, pairs=((2, 0), (3, 1), (0, 2), (1, 3))):
-            for a, b in pairs:
-                self.step(k, a, "u")
-                self.step(k, b, "d")
-
-        def wave1(self):
-            self.step(1, 0, "u")
-            self.step(1, 2, "d")
-            self.step(1, 1, "u")
-            self.step(1, 3, "d")
-
-        def final(self, h):
-            total = self.own(z, h)
-            for way in ("u", "d"):
-                _, got, device = self.side[way]
-                recv(got.at[3, head(h)], (self.tag, way, 3, h), device)
-                total = total + got[3, head(h), :].astype(F32)
-            return total
+    rs_d.wave1()
 
     for j in (1, 3, 2):
-        src = yp(-j)
-        recv(bb.at[src, c], ("b", j), d_y[j])
-        send(bb.at[src, c], bb.at[src, c], ("b2", j), d_sib)
-
-    uacc[...] = jnp.zeros_like(uacc)
-    for j in (1, 2, 3):
-
-        @pl.when(y + j < NY)
-        def _(j=j):
-            recv(urecv.at[j - 1], ("u", j), d_y[4 - j])
-            uacc[...] += urecv[j - 1].astype(F32)
-
-    def own_d(zd, h):
-        far = lax.div(z, 4) != lax.div(zd, 4)
-        mid = lax.div(z, 2) != lax.div(zd, 2)
-        level = jnp.where(far, 2, jnp.where(mid, 1, 0))
-        on = (z > zd).astype(F32)
-        return uacc[head(h), :] + on * st[level, head(h), :]
-
-    rs_d = Scatter("d", own_d, du, dd, ru, rd)
-    rs_d.start(0)
-    rs_d.start(1)
+        recv(bb.at[j, c], ("b", j), d_y[j])
+        send(bb.at[j, c], bb.at[j, c], ("b2",), d_sib)
 
     s34[...] = jnp.zeros_like(s34)
-    for i in (0, 1):
-        part = pl.ds(HALF * i, HALF)
+    for h in range(HH):
         for j in (1, 2, 3):
 
             @pl.when(y >= j)
             def _(j=j):
                 which = 1 - near if j == 1 else 1
-                recv(trecv.at[j - 1, part], ("t", j, i), d_y[j])
-                s34[which, part, :] = s34[which, part, :] + trecv[j - 1, part, :].astype(F32)
-
-        for h in (2 * i, 2 * i + 1):
-            from_states(
-                h, [s34[0, head(h), :].astype(BF), s34[1, head(h), :].astype(BF)], (5, 6), (None, None)
-            )
-            a16 = attf[h].astype(BF)
-            att16[:, 128 * h : 128 * h + 128] = a16
-            at[y, head(h), :] = a16.T
+                recv(trecv.at[j - 1, head(h)], ("t%d" % j, h), d_y[j])
+                s34[which, head(h), :] = s34[which, head(h), :] + trecv[j - 1, head(h), :].astype(F32)
+
+        from_states(
+            h, [s34[0, head(h), :].astype(BF), s34[1, head(h), :].astype(BF)], (5, 6), (None, None)
+        )
+        a16 = attf[h].astype(BF)
+        att16[:, 128 * h : 128 * h + 128] = a16
+        at[0, head(h), :] = a16.T
         for j in (1, 3, 2):
-            send(at.at[y, part], at.at[y, part], ("at", j, i), d_y[j])
-        if i == 0:
-            rs_d.wave1()
+            send(at.at[0, head(h)], at.at[j, head(h)], ("at", h), d_y[j])
+        if h == 1:
+            rs_d.wave(2, ((2, 0), (3, 1)))
+
+    @pl.when(y > 0)
+    def _():
+        u_total(main, "u1")
+
+    @pl.when(y == 3)
+    def _():
+        u_total(0, "u2")
+
+    for j in (1, 2, 3):
+
+        @pl.when(y >= j)
+        def _(j=j):
+            which = 1 - near if j == 1 else 1
+            rcopy(us.at[which], ur.at[j - 1], ("u%dy" % j,), d_y[4 - j]).start()
 
     def m_part(index):
         cols = pl.ds(pl.multiple_of(index * 512, 512), 512)
@@ -362,16 +392,26 @@
     for i in range(NX):
         mp[0, i] = m_part(i * 2 + sib)
     send(mp.at[0], mr, ("m",), d_sib)
-    rs_d.wave(2)
+    rs_d.wave(2, ((0, 2), (1, 3)))
     for i in range(NX):
         mp[1, i] = m_part(i * 2 + c)
-    recv(mr, ("m",), d_sib)
-    for j in (1, 3, 2):
-        ms[j - 1] = (mp[1, xp(j)].astype(F32) + mr[xp(j)].astype(F32)).astype(BF)
-        send(ms.at[j - 1], mx.at[j - 1], ("mx", j), d_x[j])
-
-    for j in (1, 2, 3):
-        recv(bb.at[yp(-j), sib], ("b2", j), d_sib)
+
+    recv(bb.at[pl.ds(1, 3), sib], ("b2",), d_sib)
+
+    def later_y():
+        @pl.when(y < 3)
+        def _():
+            usum[...] = jnp.zeros_like(usum)
+            for j in (1, 2, 3):
+
+                @pl.when(y + j < NY)
+                def _(j=j):
+                    recv(ur.at[j - 1], ("u%dy" % j,), d_y[4 - j])
+                    usum[...] += ur[j - 1].astype(F32)
+
+            uall[NZ - 1] = usum[...].astype(BF)
+            for j in range(1, NZ):
+                rcopy(uall.at[NZ - 1], uall.at[j - 1], ("ua",), dev(y, up(j), x, c)).start()
 
     def own_c(zd, h):
         return cf[zd, head(h), :]
@@ -379,8 +419,8 @@
     rs_c = Scatter("c", own_c, cu, cd, xu, xd)
     for i in (0, 1):
         part = pl.ds(HALF * i, HALF)
-        for j in (1, 3, 2):
-            recv(at.at[yp(-j), part], ("at", j, i), d_y[j])
+        for h in (2 * i, 2 * i + 1):
+            recv(at.at[pl.ds(1, 3), head(h)], ("at", h), d_y[1])
         a = jnp.concatenate([at[n, part, :] for n in range(NY)], axis=1)
         for n in range(4):
             b = jnp.concatenate(
@@ -390,11 +430,28 @@
             cf[2 * n, part, :] = out[:, :128]
             cf[2 * n + 1, part, :] = out[:, 128:]
         rs_c.start(i)
-    rs_d.wave(3)
+        if i == 0:
+            rs_d.wave(3, ((2, 0), (3, 1)))
+            later_y()
+    recv(mr, ("m",), d_sib)
+    for j in (1, 3, 2):
+        ms[j - 1] = (mp[1, xp(j)].astype(F32) + mr[xp(j)].astype(F32)).astype(BF)
+        send(ms.at[j - 1], mx.at[j - 1], ("mx",), d_x[j])
+    rs_d.wave(3, ((0, 2), (1, 3)))
     rs_c.wave1()
 
-    for h in range(HH):
-        dn[head(h), :] = rs_d.final(h).astype(BF)
+    @pl.when(y < 3)
+    def _():
+        recv(uall.at[pl.ds(0, NZ - 1)], ("ua",), d_up)
+
+    @pl.when(y == 3)
+    def _():
+        uall[...] = jnp.zeros_like(uall)
+
+    for h in range(HH):
+        own_slots = [lax.rem(z - 2 * h - i + 2 * NZ - 1, NZ) for i in (0, 1)]
+        later = jnp.concatenate([uall[n] for n in own_slots], axis=0).astype(F32)
+        dn[head(h), :] = (rs_d.final(h) + later).astype(BF)
     rs_c.wave(2)
     for h in range(HH):
         place = pl.ds(h, 128, stride=HH)
@@ -403,33 +460,49 @@
         dv_o[place, :] = dv_o[place, :] + mm(kb[h], block)
 
     out = mp[1, x].astype(F32) + mr[x].astype(F32)
+    recv(mx, ("mx",), d_x[1])
     for j in (1, 3, 2):
-        recv(mx.at[j - 1], ("mx", j), d_x[j])
         out = out + mx[j - 1].astype(F32)
     mixed_o[...] = out.astype(BF)
     rs_c.wave(3)
     for h in (2, 3, 0, 1):
         pg_o[head(h), :] = rs_c.final(h)
 
-    for op in pending:
-        op.wait_send()
+    for name, ref in (
+        ("og", gf.at[pl.ds(0, 4)]), ("og2", gf.at[pl.ds(0, 3)]), ("b", gf.at[pl.ds(0, 3)]),
+        ("b2", gf.at[pl.ds(0, 3)]), ("ag", sb.at[pl.ds(0, 7)]), ("d", sb.at[pl.ds(0, 7)]),
+        ("c", sb.at[pl.ds(0, 7)]), ("at", at.at[pl.ds(0, 3)]), ("m", mr), ("mx", mx),
+    ):
+        assert group[name] == math.prod(ref.shape), (name, group[name])
+        sent(ref, name)
+
+    @pl.when(y > 0)
+    def _():
+        sent(uwr.at[0], "u1")
+
+    @pl.when(y == 3)
+    def _():
+        sent(uwr.at[0], "u2")
+
+    @pl.when(y < 3)
+    def _():
+        sent(uwr.at[0], "ua")
+
     for j in (1, 2, 3):
 
         @pl.when(y >= j)
         def _(j=j):
-            which = 1 - near if j == 1 else 1
-            rcopy(sty.at[which], urecv.at[j - 1], ids("u", j), d_y[4 - j]).wait_send()
+            sent(us.at[0], "u%dy" % j)
 
         @pl.when(y + j < NY)
         def _(j=j):
-            for i in (0, 1):
-                part = pl.ds(HALF * i, HALF)
-                rcopy(tsend.at[part], trecv.at[j - 1, part], ids("t", j, i), d_y[j]).wait_send()
-
-    assert len(ids.table) <= N_SEM, len(ids.table)
-
-
-N_SEM = 120
+            sent(tsend, "t%d" % j)
+
+    assert len(sids.table) <= S_SEM and len(ids.table) <= N_SEM, (len(sids.table), len(ids.table))
+
+
+N_SEM = 119
+S_SEM = 19
 VLIM = 28
 
 
@@ -472,13 +545,14 @@
             v((4, 128, 128), BF), v((4, 128, 128), BF), v((4, 128, 128), BF), v((4, 128, 128), BF),
             v((4, 128, 128), BF), v((4, 128, 128), BF), v((4, 128, 128), F32), v((128, 512), BF),
             v((8, 512, 128), BF), v((3, 512, 128), F32), v((2, 512, 128), BF),
-            v(blk, BF), v((3, 512, 128), BF), v((2, 512, 128), F32), v((3, 512, 128), BF), v(blk, F32),
+            v(blk, BF), v((3, 512, 128), BF), v((2, 512, 128), F32),
+            v((2, 7, 64, 128), BF), v((2, 64, 128), BF), v((3, 64, 128), BF), v((64, 128), F32), v((8, 64, 128), BF),
             v((4, 512, 128), BF), v((4, 512, 128), BF), v((4, 512, 128), BF), v((4, 512, 128), BF), v(blk, BF),
             v((4, 2, 128, 512), BF), v((4, 512, 128), BF), v((8, 512, 128), F32),
             v((4, 512, 128), BF), v((4, 512, 128), BF), v((4, 512, 128), BF), v((4, 512, 128), BF),
             v((2, 4, 128, 512), BF), v((4, 128, 512), BF), v((3, 128, 512), BF), v((3, 128, 512), BF),
-            pltpu.SemaphoreType.DMA((12,)),
-            pltpu.SemaphoreType.DMA((N_SEM,)),
+            pltpu.SemaphoreType.DMA((6,)),
+            pltpu.SemaphoreType.DMA((S_SEM,)),
             pltpu.SemaphoreType.DMA((N_SEM,)),
         ],
         compiler_params=pltpu.CompilerParams(

time: 60.1 us -> 57.1 us (0.950)
  Pallas kernels: 58.4 us -> 55.5 us
    pallas_call x1, Pallas kernels: 57 us -> 54.2 us  [body(): pl.pallas_call(body_kernel, out_shape=(jax.ShapeDtypeStruct((128, 512), B...]
where the time goes in v3:
time: 57.1 us; the launch traced here: 56.2 us
  Pallas kernels  55.5 us (97%)
  between operations  0.64 us (1%)
    pallas_call x1, Pallas kernels, body(): pl.pallas_call(body_kernel, out_shape=(jax.ShapeDtypeStruct((128, 512), B...  54.2 us
    pallas_call x1, Pallas kernels, body(): pl.pallas_call(out_kernel, out_shape=tuple((jax.ShapeDtypeStruct(o.shape,...  1.34 us

profile of v3, /device:TPU:8, one launch (start us, length us, event | category | flops | bytes accessed | tf_op | source)
XLA Modules:
  0.0 56.2 jit_solution(12384233892135524345)
XLA Ops:
  0.6 54.2 %log_linear.1 = (bf16[128,512]{1,0:T(8,128)(2,1)S(1)}, f32[512,128]{1,0:T(8,128)S(1)}, f32[512,128]{1,0:T(8,128)S(1)}, f32[512,128]{1,0:T(8,128)S(1)}, f32[512,128]{1,0:T(8,128)S(1)}) custom-call(f32[512,128]{1,0:T(8,128)} %bitcast.6, f32[512,128]{1,0:T(8,128)} %bitcast.7, f32[512,128]{1,0:T(8,128)} %bitcast.8, f32[7,4,128]{2,1,0:T(4,128)} %lam_h.1, ...), custom_call_target="tpu_custom_call" | custom-call | tf_op jit(solution)/shard_map/log_linear/pallas_call | solution.py:530
  54.8 1.3 %results.1 = (bf16[128,512]{1,0:T(8,128)(2,1)}, f32[512,128]{1,0:T(8,128)}, f32[512,128]{1,0:T(8,128)}, f32[512,128]{1,0:T(8,128)}, f32[512,128]{1,0:T(8,128)}) custom-call(bf16[128,512]{1,0:T(8,128)(2,1)S(1)} %get-tuple-element.15.refs_0_, f32[512,128]{1,0:T(8,128)S(1)} %get-tuple-element.16.refs_1_, f32[512,128]{1,0:T(8,128)S(1)} %get-tuple-element.17.refs_2_, ...), custom_call_target="tpu_custom_call" | custom-call | tf_op jit(solution)/shard_map/results/pallas_call | solution.py:563

commit v4 on v3

--- a/solution.py
+++ b/solution.py
@@ -36,8 +36,8 @@
     mixed_o, dq_o, dk_o, dv_o, pg_o,
     qf, kf, vf, lam_v, lam_s, lam_t, wo, gf, gacc,
     qb, kb, vb, gb, pb, db, attf, att16,
-    sb, st, sty, tsend, trecv, s34, uwr, us, ur, usum, uall,
-    du, dd, ru, rd, dn,
+    sb, st, sty, tsend, trecv, tsum, uwr, uwl, us, us2, ur, usum, uo, uall,
+    dch, dnear, dsum, dfin,
     bb, at, cf, cu, cd, xu, xd,
     mp, mr, ms, mx,
     lsem, ssem, rsem,
@@ -196,22 +196,29 @@
     og_relay(2)
     for j in (1, 2, 3):
         send(gf.at[yp(j) * 2 + c], bb.at[j, c], ("b", j), d_y[j])
+    ag_relay(2, (2, 3))
     for j in (1, 3, 2):
         gacc[...] += g_part(xp(-j) * 2 + c)
-    ag_relay(2, (2, 3))
-    for j in (1, 3, 2):
+
+    def g_far(j):
         src = xp(-j) * 2 + sib
         recv(gf.at[src], ("og2", j), d_sib)
         gacc[...] += g_part(src)
+
+    g_far(1)
+    g_far(3)
+    ag_relay(3, (0, 1))
+    g_far(2)
     for h in range(HH):
         gb[h] = gacc[:, 128 * h : 128 * h + 128].astype(BF)
+    ag_relay(3, (2, 3))
 
     def weighted(h, level):
         return (qb[h].astype(F32) * lam(level, h)).astype(BF)
 
-    for d in (4, 3):
+    for d in (4, 3, 2):
         for h in range(HH):
-            sty[d - 3, head(h), :] = mm(weighted(h, 2 + d), gb[h], TN).astype(BF)
+            sty[{3: 0, 4: 1, 2: 2}[d], head(h), :] = mm(weighted(h, 2 + d), gb[h], TN).astype(BF)
     near = lax.rem(y, 2)
     main = jnp.where(y == 1, 0, 1)
 
@@ -230,11 +237,42 @@
             total = total + uwr[level, j - 1].astype(F32)
         us[level] = total.astype(BF)
 
-    ag_relay(3)
-
-    for d in (0, 1, 2):
+    def half_sum():
+        for j in range(1, NZ):
+            to = up(j)
+            rcopy(sty.at[2, piece(to)], uwl.at[z - 4], ("u0",), dev(y, to, x, c)).start()
+
+    def half_total():
+        @pl.when(z < 4)
+        def _():
+            recv(uwl, ("u0",), d_up)
+
+        @pl.when(z >= 4)
+        def _():
+            uwl[z - 4] = sty[2, piece(z), :]
+            recv(uwl.at[pl.ds(0, 3)], ("u0",), d_up)
+
+        us2[...] = sum(uwl[i].astype(F32) for i in range(4))
+
+
+    for d in (1, 0):
         for h in range(HH):
-            st[d, head(h), :] = mm(weighted(h, 2 + d), gb[h], TN)
+            st[d, head(h), :] = mm(weighted(h, 2 + d), gb[h], TN).astype(BF)
+
+    place4 = lax.rem(z, 4)
+
+    @pl.when(place4 == 3)
+    def _():
+        for h in range(HH):
+            rcopy(st.at[1, head(h)], dch.at[head(h)], ("d", h), d_dn).start()
+        rcopy(st.at[0], dnear, ("d0",), d_dn).start()
+
+    def chain(level):
+        for h in range(HH):
+            recv(dch.at[head(h)], ("d", h), d_dn)
+            total = dch[head(h), :].astype(F32) + st[level, head(h), :].astype(F32)
+            dsum[head(h), :] = total.astype(BF)
+            rcopy(dsum.at[head(h)], dch.at[head(h)], ("d", h), d_dn).start()
 
     class Scatter:
         def __init__(self, tag, own, bu, bd, pu, pd):
@@ -255,19 +293,13 @@
         def start(self, i):
             for h in (2 * i, 2 * i + 1):
                 self.step(0, h, "ud"[i])
+                self.step(1, h, "du"[i])
+
+        def wave(self, i, k):
             for h in (2 * i, 2 * i + 1):
-                self.step(1, h, "du"[i])
-
-        def wave(self, k, pairs=((2, 0), (3, 1), (0, 2), (1, 3))):
-            for a, b in pairs:
-                self.step(k, a, "u")
-                self.step(k, b, "d")
-
-        def wave1(self):
-            self.step(1, 0, "u")
-            self.step(1, 2, "d")
-            self.step(1, 1, "u")
-            self.step(1, 3, "d")
+                self.step(k, h, "ud"[i])
+                if k < 3:
+                    self.step(k + 1, h, "du"[i])
 
         def final(self, h):
             total = self.own(z, h)
@@ -277,16 +309,6 @@
                 total = total + got[3, head(h), :].astype(F32)
             return total
 
-    def own_d(zd, h):
-        far = lax.div(z, 4) != lax.div(zd, 4)
-        mid = lax.div(z, 2) != lax.div(zd, 2)
-        level = jnp.where(far, 2, jnp.where(mid, 1, 0))
-        on = (z > zd).astype(F32)
-        return on * st[level, head(h), :]
-
-    rs_d = Scatter("d", own_d, du, dd, ru, rd)
-    rs_d.start(0)
-    rs_d.start(1)
     for i in (0, 1):
         bb[0, i] = gf[y * 2 + i]
 
@@ -296,11 +318,14 @@
         for n in range(1, NZ):
             total = total + sb[n, head(h), :].astype(F32)
         tsend[head(h), :] = total.astype(BF)
-        for j in (1, 2, 3):
-
-            @pl.when(y + j < NY)
-            def _(j=j):
-                rcopy(tsend.at[head(h)], trecv.at[j - 1, head(h)], ("t%d" % j, h), d_y[j]).start()
+
+        @pl.when((y == 0) | (y == 2))
+        def _(h=h):
+            rcopy(tsend.at[head(h)], trecv.at[0, head(h)], ("t", h), d_y[1]).start()
+
+        @pl.when(y == 1)
+        def _(h=h):
+            rcopy(tsend.at[head(h)], trecv.at[0, head(h)], ("t", h), d_y[3]).start()
 
     @pl.when(y > 0)
     def _():
@@ -309,12 +334,31 @@
     @pl.when(y == 3)
     def _():
         u_sum(0, "u2")
+
+    @pl.when(z >= 4)
+    def _():
+        half_sum()
 
     for h in range(HH):
         db[h] = (mm(gb[h], vb[h], NT) * weight(h)).astype(BF)
         dq_o[pl.ds(h, 128, stride=HH), :] = mm(db[h], kb[h])
         dk_o[pl.ds(h, 128, stride=HH), :] = mm(db[h], qb[h], TN)
         dv_o[pl.ds(h, 128, stride=HH), :] = mm(pb[h], gb[h], TN)
+
+    @pl.when(y < 2)
+    def _():
+        for h in range(HH):
+            recv(trecv.at[0, head(h)], ("t", h), d_y[1])
+            both = tsend[head(h), :].astype(F32) + trecv[0, head(h), :].astype(F32)
+            tsum[head(h), :] = both.astype(BF)
+
+            @pl.when(y == 1)
+            def _(h=h):
+                rcopy(tsum.at[head(h)], trecv.at[1, head(h)], ("tt", h), d_y[1]).start()
+
+            @pl.when(y == 0)
+            def _(h=h):
+                rcopy(tsum.at[head(h)], trecv.at[1, head(h)], ("tt", h), d_y[3]).start()
 
     z1 = z + 1 - 2 * lax.rem(z, 2)
     zp = lax.div(z, 2)
@@ -343,47 +387,46 @@
             quad = quad + sb[zq1 + i, head(h), :].astype(F32)
         from_states(h, [sb[z1, head(h), :], pair, quad.astype(BF)], (2, 3, 4), (b0, b1, b2))
 
-    rs_d.wave1()
-
     for j in (1, 3, 2):
         recv(bb.at[j, c], ("b", j), d_y[j])
         send(bb.at[j, c], bb.at[j, c], ("b2",), d_sib)
 
-    s34[...] = jnp.zeros_like(s34)
-    for h in range(HH):
-        for j in (1, 2, 3):
-
-            @pl.when(y >= j)
-            def _(j=j):
-                which = 1 - near if j == 1 else 1
-                recv(trecv.at[j - 1, head(h)], ("t%d" % j, h), d_y[j])
-                s34[which, head(h), :] = s34[which, head(h), :] + trecv[j - 1, head(h), :].astype(F32)
-
-        from_states(
-            h, [s34[0, head(h), :].astype(BF), s34[1, head(h), :].astype(BF)], (5, 6), (None, None)
-        )
+    @pl.when(place4 == 2)
+    def _():
+        chain(1)
+
+    @pl.when(y == 0)
+    def _():
+        trecv[...] = jnp.zeros_like(trecv)
+
+    @pl.when(y == 1)
+    def _():
+        trecv[1] = jnp.zeros_like(tsend)
+
+    @pl.when(y == 2)
+    def _():
+        trecv[0] = jnp.zeros_like(tsend)
+
+    for h in range(HH):
+
+        @pl.when(y == 3)
+        def _(h=h):
+            recv(trecv.at[0, head(h)], ("t", h), d_y[1])
+
+        @pl.when(y >= 2)
+        def _(h=h):
+            recv(trecv.at[1, head(h)], ("tt", h), d_y[1])
+
+        from_states(h, [trecv[0, head(h), :], trecv[1, head(h), :]], (5, 6), (None, None))
         a16 = attf[h].astype(BF)
         att16[:, 128 * h : 128 * h + 128] = a16
         at[0, head(h), :] = a16.T
         for j in (1, 3, 2):
             send(at.at[0, head(h)], at.at[j, head(h)], ("at", h), d_y[j])
-        if h == 1:
-            rs_d.wave(2, ((2, 0), (3, 1)))
-
-    @pl.when(y > 0)
-    def _():
-        u_total(main, "u1")
-
-    @pl.when(y == 3)
-    def _():
-        u_total(0, "u2")
-
-    for j in (1, 2, 3):
-
-        @pl.when(y >= j)
-        def _(j=j):
-            which = 1 - near if j == 1 else 1
-            rcopy(us.at[which], ur.at[j - 1], ("u%dy" % j,), d_y[4 - j]).start()
+
+    @pl.when(place4 == 1)
+    def _():
+        chain(0)
 
     def m_part(index):
         cols = pl.ds(pl.multiple_of(index * 512, 512), 512)
@@ -392,32 +435,15 @@
     for i in range(NX):
         mp[0, i] = m_part(i * 2 + sib)
     send(mp.at[0], mr, ("m",), d_sib)
-    rs_d.wave(2, ((0, 2), (1, 3)))
     for i in range(NX):
         mp[1, i] = m_part(i * 2 + c)
 
-    recv(bb.at[pl.ds(1, 3), sib], ("b2",), d_sib)
-
-    def later_y():
-        @pl.when(y < 3)
-        def _():
-            usum[...] = jnp.zeros_like(usum)
-            for j in (1, 2, 3):
-
-                @pl.when(y + j < NY)
-                def _(j=j):
-                    recv(ur.at[j - 1], ("u%dy" % j,), d_y[4 - j])
-                    usum[...] += ur[j - 1].astype(F32)
-
-            uall[NZ - 1] = usum[...].astype(BF)
-            for j in range(1, NZ):
-                rcopy(uall.at[NZ - 1], uall.at[j - 1], ("ua",), dev(y, up(j), x, c)).start()
-
     def own_c(zd, h):
         return cf[zd, head(h), :]
 
     rs_c = Scatter("c", own_c, cu, cd, xu, xd)
-    for i in (0, 1):
+
+    def product(i):
         part = pl.ds(HALF * i, HALF)
         for h in (2 * i, 2 * i + 1):
             recv(at.at[pl.ds(1, 3), head(h)], ("at", h), d_y[1])
@@ -430,47 +456,122 @@
             cf[2 * n, part, :] = out[:, :128]
             cf[2 * n + 1, part, :] = out[:, 128:]
         rs_c.start(i)
-        if i == 0:
-            rs_d.wave(3, ((2, 0), (3, 1)))
-            later_y()
+
+    recv(bb.at[pl.ds(1, 3), sib], ("b2",), d_sib)
+    product(0)
+
+    def u_send(j, level):
+        rcopy(us.at[level], ur.at[j - 1], ("u%dy" % j,), d_y[4 - j]).start()
+
+    @pl.when(y > 0)
+    def _():
+        u_total(main, "u1")
+
+    @pl.when(y == 1)
+    def _():
+        u_send(1, 0)
+
+    @pl.when(y == 2)
+    def _():
+        u_send(1, 1)
+        u_send(2, 1)
+
+    @pl.when(y == 3)
+    def _():
+        u_send(2, 1)
+        u_send(3, 1)
+
+    product(1)
     recv(mr, ("m",), d_sib)
     for j in (1, 3, 2):
         ms[j - 1] = (mp[1, xp(j)].astype(F32) + mr[xp(j)].astype(F32)).astype(BF)
         send(ms.at[j - 1], mx.at[j - 1], ("mx",), d_x[j])
-    rs_d.wave(3, ((0, 2), (1, 3)))
-    rs_c.wave1()
-
-    @pl.when(y < 3)
-    def _():
-        recv(uall.at[pl.ds(0, NZ - 1)], ("ua",), d_up)
+    rs_c.wave(0, 1)
 
     @pl.when(y == 3)
     def _():
-        uall[...] = jnp.zeros_like(uall)
-
-    for h in range(HH):
-        own_slots = [lax.rem(z - 2 * h - i + 2 * NZ - 1, NZ) for i in (0, 1)]
-        later = jnp.concatenate([uall[n] for n in own_slots], axis=0).astype(F32)
-        dn[head(h), :] = (rs_d.final(h) + later).astype(BF)
-    rs_c.wave(2)
-    for h in range(HH):
-        place = pl.ds(h, 128, stride=HH)
-        block = dn[head(h), :]
-        dk_o[place, :] = dk_o[place, :] + mm(vb[h], block, NT)
-        dv_o[place, :] = dv_o[place, :] + mm(kb[h], block)
+        u_total(0, "u2")
+        u_send(1, 0)
+
+    half_total()
+
+    rs_c.wave(1, 1)
+
+    def later_all():
+        usum[...] = jnp.zeros_like(usum)
+        for j in (1, 2, 3):
+
+            @pl.when(y + j < NY)
+            def _(j=j):
+                recv(ur.at[j - 1], ("u%dy" % j,), d_y[4 - j])
+                usum[...] += ur[j - 1].astype(F32)
+
+        uo[0] = usum[...].astype(BF)
+        uo[1] = (usum[...] + us2[...]).astype(BF)
+        uall[NZ - 1] = uo[jnp.where(z < 4, 1, 0)]
+        for j in range(1, NZ):
+            to = up(j)
+
+            @pl.when((y < 3) | (to < 4))
+            def _(j=j, to=to):
+                low = jnp.where(to < 4, 1, 0)
+                rcopy(uo.at[low], uall.at[j - 1], ("ua",), dev(y, to, x, c)).start()
+
+    later_all()
+    rs_c.wave(0, 2)
+    rs_c.wave(1, 2)
+    rs_c.wave(0, 3)
+    rs_c.wave(1, 3)
 
     out = mp[1, x].astype(F32) + mr[x].astype(F32)
     recv(mx, ("mx",), d_x[1])
     for j in (1, 3, 2):
         out = out + mx[j - 1].astype(F32)
     mixed_o[...] = out.astype(BF)
-    rs_c.wave(3)
-    for h in (2, 3, 0, 1):
+
+    some = (y < 3) | (z < 4)
+
+    @pl.when(some)
+    def _():
+        recv(uall.at[pl.ds(0, NZ - 1)], ("ua",), d_up)
+
+    @pl.when(jnp.logical_not(some))
+    def _():
+        uall[...] = jnp.zeros_like(uall)
+
+    @pl.when(place4 == 0)
+    def _():
+        for h in range(HH):
+            recv(dch.at[head(h)], ("d", h), d_dn)
+        dfin[...] = dch[...]
+
+    @pl.when(place4 == 1)
+    def _():
+        dfin[...] = dch[...]
+
+    @pl.when(place4 == 2)
+    def _():
+        recv(dnear, ("d0",), d_dn)
+        dfin[...] = dnear[...]
+
+    @pl.when(place4 == 3)
+    def _():
+        dfin[...] = jnp.zeros_like(dfin)
+
+    for h in range(HH):
+        own_slots = [lax.rem(z - 2 * h - i + 2 * NZ - 1, NZ) for i in (0, 1)]
+        later = jnp.concatenate([uall[n] for n in own_slots], axis=0).astype(F32)
+        block = (dfin[head(h), :].astype(F32) + later).astype(BF)
+        place = pl.ds(h, 128, stride=HH)
+        dk_o[place, :] = dk_o[place, :] + mm(vb[h], block, NT)
+        dv_o[place, :] = dv_o[place, :] + mm(kb[h], block)
+
+    for h in (0, 1, 2, 3):
         pg_o[head(h), :] = rs_c.final(h)
 
     for name, ref in (
         ("og", gf.at[pl.ds(0, 4)]), ("og2", gf.at[pl.ds(0, 3)]), ("b", gf.at[pl.ds(0, 3)]),
-        ("b2", gf.at[pl.ds(0, 3)]), ("ag", sb.at[pl.ds(0, 7)]), ("d", sb.at[pl.ds(0, 7)]),
+        ("b2", gf.at[pl.ds(0, 3)]), ("ag", sb.at[pl.ds(0, 7)]),
         ("c", sb.at[pl.ds(0, 7)]), ("at", at.at[pl.ds(0, 3)]), ("m", mr), ("mx", mx),
     ):
         assert group[name] == math.prod(ref.shape), (name, group[name])
@@ -488,21 +589,45 @@
     def _():
         sent(uwr.at[0], "ua")
 
+    @pl.when((y == 3) & (z < 4))
+    def _():
+        sent(uwl.at[pl.ds(0, 3)], "ua")
+
+    @pl.when((y == 3) & (z >= 4))
+    def _():
+        sent(uwl, "ua")
+
+    @pl.when(z >= 4)
+    def _():
+        sent(uwr.at[0], "u0")
+
+    @pl.when(place4 > 0)
+    def _():
+        sent(dch, "d")
+
+    @pl.when(place4 == 3)
+    def _():
+        sent(dnear, "d0")
+
+    @pl.when(y < 3)
+    def _():
+        sent(tsend, "t")
+
+    @pl.when(y < 2)
+    def _():
+        sent(tsend, "tt")
+
     for j in (1, 2, 3):
 
         @pl.when(y >= j)
         def _(j=j):
             sent(us.at[0], "u%dy" % j)
 
-        @pl.when(y + j < NY)
-        def _(j=j):
-            sent(tsend, "t%d" % j)
-
     assert len(sids.table) <= S_SEM and len(ids.table) <= N_SEM, (len(sids.table), len(ids.table))
 
 
-N_SEM = 119
-S_SEM = 19
+N_SEM = 97
+S_SEM = 21
 VLIM = 28
 
 
@@ -544,10 +669,11 @@
             v((512, 4096), BF), v((8, 128, 512), BF), v((128, 512), F32),
             v((4, 128, 128), BF), v((4, 128, 128), BF), v((4, 128, 128), BF), v((4, 128, 128), BF),
             v((4, 128, 128), BF), v((4, 128, 128), BF), v((4, 128, 128), F32), v((128, 512), BF),
-            v((8, 512, 128), BF), v((3, 512, 128), F32), v((2, 512, 128), BF),
-            v(blk, BF), v((3, 512, 128), BF), v((2, 512, 128), F32),
-            v((2, 7, 64, 128), BF), v((2, 64, 128), BF), v((3, 64, 128), BF), v((64, 128), F32), v((8, 64, 128), BF),
-            v((4, 512, 128), BF), v((4, 512, 128), BF), v((4, 512, 128), BF), v((4, 512, 128), BF), v(blk, BF),
+            v((8, 512, 128), BF), v((2, 512, 128), BF), v((3, 512, 128), BF),
+            v(blk, BF), v((2, 512, 128), BF), v(blk, BF),
+            v((2, 7, 64, 128), BF), v((4, 64, 128), BF), v((2, 64, 128), BF), v((64, 128), F32), v((3, 64, 128), BF),
+            v((64, 128), F32), v((2, 64, 128), BF), v((8, 64, 128), BF),
+            v(blk, BF), v(blk, BF), v(blk, BF), v(blk, BF),
             v((4, 2, 128, 512), BF), v((4, 512, 128), BF), v((8, 512, 128), F32),
             v((4, 512, 128), BF), v((4, 512, 128), BF), v((4, 512, 128), BF), v((4, 512, 128), BF),
             v((2, 4, 128, 512), BF), v((4, 128, 512), BF), v((3, 128, 512), BF), v((3, 128, 512), BF),

time: 57.1 us -> 54.1 us (0.947)
  Pallas kernels: 55.5 us -> 52.9 us
    pallas_call x1, Pallas kernels: 54.2 us -> 51.5 us  [body(): pl.pallas_call(body_kernel, out_shape=(jax.ShapeDtypeStruct((128, 512), B...]
where the time goes in v4:
time: 54.1 us; the launch traced here: 53.5 us
  Pallas kernels  52.9 us (98%)
  between operations  0.64 us (1%)
    pallas_call x1, Pallas kernels, body(): pl.pallas_call(body_kernel, out_shape=(jax.ShapeDtypeStruct((128, 512), B...  51.5 us
    pallas_call x1, Pallas kernels, body(): pl.pallas_call(out_kernel, out_shape=tuple((jax.ShapeDtypeStruct(o.shape,...  1.34 us

profile of v4, /device:TPU:8, one launch (start us, length us, event | category | flops | bytes accessed | tf_op | source)
XLA Modules:
  0.0 53.5 jit_solution(13952486569456448323)
XLA Ops:
  0.6 51.5 %log_linear.1 = (bf16[128,512]{1,0:T(8,128)(2,1)S(1)}, f32[512,128]{1,0:T(8,128)S(1)}, f32[512,128]{1,0:T(8,128)S(1)}, f32[512,128]{1,0:T(8,128)S(1)}, f32[512,128]{1,0:T(8,128)S(1)}) custom-call(f32[512,128]{1,0:T(8,128)} %bitcast.6, f32[512,128]{1,0:T(8,128)} %bitcast.7, f32[512,128]{1,0:T(8,128)} %bitcast.8, f32[7,4,128]{2,1,0:T(4,128)} %lam_h.1, ...), custom_call_target="tpu_custom_call" | custom-call | tf_op jit(solution)/shard_map/log_linear/pallas_call | solution.py:655
  52.2 1.3 %results.1 = (bf16[128,512]{1,0:T(8,128)(2,1)}, f32[512,128]{1,0:T(8,128)}, f32[512,128]{1,0:T(8,128)}, f32[512,128]{1,0:T(8,128)}, f32[512,128]{1,0:T(8,128)}) custom-call(bf16[128,512]{1,0:T(8,128)(2,1)S(1)} %get-tuple-element.15.refs_0_, f32[512,128]{1,0:T(8,128)S(1)} %get-tuple-element.16.refs_1_, f32[512,128]{1,0:T(8,128)S(1)} %get-tuple-element.17.refs_2_, ...), custom_call_target="tpu_custom_call" | custom-call | tf_op jit(solution)/shard_map/results/pallas_call | solution.py:689

commit v5 on v4

--- a/solution.py
+++ b/solution.py
@@ -114,18 +114,6 @@
 
     loads["k"].wait()
     loads["v"].wait()
-    for h in range(HH):
-        kh = rows(kf, h).astype(BF)
-        vh = rows(vf, h).astype(BF)
-        kb[h] = kh
-        vb[h] = vh
-        sb[z, head(h), :] = mm(kh, vh, TN).astype(BF)
-
-    pl.semaphore_wait(barrier, len(partners))
-
-    for j in (1, 3, 2):
-        send(og_h, gf.at[hd], ("og", j), d_x[j])
-
     def ag_send(k, h):
         su, sd = up(-k), up(k)
         if k < 3 or h < 2:
@@ -144,7 +132,23 @@
             ag_recv(k - 1, h)
             ag_send(k, h)
 
-    for h in range(HH):
+    def key_value_sum(h):
+        kh = rows(kf, h).astype(BF)
+        vh = rows(vf, h).astype(BF)
+        kb[h] = kh
+        vb[h] = vh
+        sb[z, head(h), :] = mm(kh, vh, TN).astype(BF)
+
+    key_value_sum(0)
+    pl.semaphore_wait(barrier, len(partners))
+    ag_send(0, 0)
+    key_value_sum(1)
+    ag_send(0, 1)
+
+    for j in (1, 3, 2):
+        send(og_h, gf.at[hd], ("og", j), d_x[j])
+    for h in (2, 3):
+        key_value_sum(h)
         ag_send(0, h)
     send(og_h, gf.at[hd], ("og", 0), d_sib)
 
@@ -192,11 +196,10 @@
     gacc[...] += g_part(x * 2 + sib)
     og_relay(1)
     og_relay(3)
-    ag_relay(2, (0, 1))
+    ag_relay(2)
     og_relay(2)
     for j in (1, 2, 3):
         send(gf.at[yp(j) * 2 + c], bb.at[j, c], ("b", j), d_y[j])
-    ag_relay(2, (2, 3))
     for j in (1, 3, 2):
         gacc[...] += g_part(xp(-j) * 2 + c)
 
@@ -254,6 +257,24 @@
 
         us2[...] = sum(uwl[i].astype(F32) for i in range(4))
 
+
+    def level_sum(h):
+        ag_recv(3, h)
+        total = sb[0, head(h), :].astype(F32)
+        for n in range(1, NZ):
+            total = total + sb[n, head(h), :].astype(F32)
+        tsend[head(h), :] = total.astype(BF)
+
+        @pl.when((y == 0) | (y == 2))
+        def _():
+            rcopy(tsend.at[head(h)], trecv.at[0, head(h)], ("t", h), d_y[1]).start()
+
+        @pl.when(y == 1)
+        def _():
+            rcopy(tsend.at[head(h)], trecv.at[0, head(h)], ("t", h), d_y[3]).start()
+
+    level_sum(0)
+    level_sum(1)
 
     for d in (1, 0):
         for h in range(HH):
@@ -312,20 +333,8 @@
     for i in (0, 1):
         bb[0, i] = gf[y * 2 + i]
 
-    for h in range(HH):
-        ag_recv(3, h)
-        total = sb[0, head(h), :].astype(F32)
-        for n in range(1, NZ):
-            total = total + sb[n, head(h), :].astype(F32)
-        tsend[head(h), :] = total.astype(BF)
-
-        @pl.when((y == 0) | (y == 2))
-        def _(h=h):
-            rcopy(tsend.at[head(h)], trecv.at[0, head(h)], ("t", h), d_y[1]).start()
-
-        @pl.when(y == 1)
-        def _(h=h):
-            rcopy(tsend.at[head(h)], trecv.at[0, head(h)], ("t", h), d_y[3]).start()
+    level_sum(2)
+    level_sum(3)
 
     @pl.when(y > 0)
     def _():
@@ -421,7 +430,7 @@
         a16 = attf[h].astype(BF)
         att16[:, 128 * h : 128 * h + 128] = a16
         at[0, head(h), :] = a16.T
-        for j in (1, 3, 2):
+        for j in (2, 1, 3):
             send(at.at[0, head(h)], at.at[j, head(h)], ("at", h), d_y[j])
 
     @pl.when(place4 == 1)
@@ -482,11 +491,11 @@
         u_send(3, 1)
 
     product(1)
+    rs_c.wave(0, 1)
     recv(mr, ("m",), d_sib)
     for j in (1, 3, 2):
         ms[j - 1] = (mp[1, xp(j)].astype(F32) + mr[xp(j)].astype(F32)).astype(BF)
         send(ms.at[j - 1], mx.at[j - 1], ("mx",), d_x[j])
-    rs_c.wave(0, 1)
 
     @pl.when(y == 3)
     def _():
@@ -496,6 +505,8 @@
     half_total()
 
     rs_c.wave(1, 1)
+
+    rs_c.wave(0, 2)
 
     def later_all():
         usum[...] = jnp.zeros_like(usum)
@@ -518,8 +529,8 @@
                 rcopy(uo.at[low], uall.at[j - 1], ("ua",), dev(y, to, x, c)).start()
 
     later_all()
-    rs_c.wave(0, 2)
     rs_c.wave(1, 2)
+
     rs_c.wave(0, 3)
     rs_c.wave(1, 3)
 

time: 54.1 us -> 55 us (1.017)
    pallas_call x1, Pallas kernels: 51.5 us -> 52.1 us  [body(): pl.pallas_call(body_kernel, out_shape=(jax.ShapeDtypeStruct((128, 512), B...]
where the time goes in v5:
time: 55 us; the launch traced here: 54.1 us
  Pallas kernels  53.4 us (97%)
  between operations  0.64 us (1%)
    pallas_call x1, Pallas kernels, body(): pl.pallas_call(body_kernel, out_shape=(jax.ShapeDtypeStruct((128, 512), B...  52.1 us
    pallas_call x1, Pallas kernels, body(): pl.pallas_call(out_kernel, out_shape=tuple((jax.ShapeDtypeStruct(o.shape,...  1.34 us

profile of v5, /device:TPU:8, one launch (start us, length us, event | category | flops | bytes accessed | tf_op | source)
XLA Modules:
  0.0 54.1 jit_solution(12300110941724236253)
XLA Ops:
  0.6 52.1 %log_linear.1 = (bf16[128,512]{1,0:T(8,128)(2,1)S(1)}, f32[512,128]{1,0:T(8,128)S(1)}, f32[512,128]{1,0:T(8,128)S(1)}, f32[512,128]{1,0:T(8,128)S(1)}, f32[512,128]{1,0:T(8,128)S(1)}) custom-call(f32[512,128]{1,0:T(8,128)} %bitcast.6, f32[512,128]{1,0:T(8,128)} %bitcast.7, f32[512,128]{1,0:T(8,128)} %bitcast.8, f32[7,4,128]{2,1,0:T(4,128)} %lam_h.1, ...), custom_call_target="tpu_custom_call" | custom-call | tf_op jit(solution)/shard_map/log_linear/pallas_call | solution.py:666
  52.8 1.3 %results.1 = (bf16[128,512]{1,0:T(8,128)(2,1)}, f32[512,128]{1,0:T(8,128)}, f32[512,128]{1,0:T(8,128)}, f32[512,128]{1,0:T(8,128)}, f32[512,128]{1,0:T(8,128)}) custom-call(bf16[128,512]{1,0:T(8,128)(2,1)S(1)} %get-tuple-element.15.refs_0_, f32[512,128]{1,0:T(8,128)S(1)} %get-tuple-element.16.refs_1_, f32[512,128]{1,0:T(8,128)S(1)} %get-tuple-element.17.refs_2_, ...), custom_call_target="tpu_custom_call" | custom-call | tf_op jit(solution)/shard_map/results/pallas_call | solution.py:700

commit v6 on v4

--- a/solution.py
+++ b/solution.py
@@ -632,16 +632,11 @@
 
 
 def out_kernel(*refs):
-    src, dst, via = refs[:5], refs[5:10], refs[10:15]
-    isem, osem = refs[15:]
-    ins = [pltpu.make_async_copy(a, b, isem.at[i]) for i, (a, b) in enumerate(zip(src, via))]
-    outs = [pltpu.make_async_copy(a, b, osem.at[i]) for i, (a, b) in enumerate(zip(via, dst))]
-    for op in ins:
+    src, dst, sem = refs[:5], refs[5:10], refs[10]
+    copies = [pltpu.make_async_copy(a, b, sem.at[i]) for i, (a, b) in enumerate(zip(src, dst))]
+    for op in copies:
         op.start()
-    for a, b in zip(ins, outs):
-        a.wait()
-        b.start()
-    for op in outs:
+    for op in copies:
         op.wait()
 
 
@@ -691,8 +686,7 @@
         out_shape=tuple(jax.ShapeDtypeStruct(o.shape, o.dtype) for o in outs),
         in_specs=[any_spec] * 5,
         out_specs=[any_spec] * 5,
-        scratch_shapes=[v(o.shape, o.dtype) for o in outs]
-        + [pltpu.SemaphoreType.DMA((5,)), pltpu.SemaphoreType.DMA((5,))],
+        scratch_shapes=[pltpu.SemaphoreType.DMA((5,))],
         compiler_params=pltpu.CompilerParams(vmem_limit_bytes=4 << 20),
         name="results",
     )(*outs)

time: 54.1 us -> 53.8 us (level)
  no operation moved by 1% of the time
where the time goes in v6:
time: 53.8 us; the launch traced here: 53.2 us
  Pallas kernels  52.6 us (98%)
  between operations  0.64 us (1%)
    pallas_call x1, Pallas kernels, body(): pl.pallas_call(body_kernel, out_shape=(jax.ShapeDtypeStruct((128, 512), B...  51.5 us

profile of v6, /device:TPU:8, one launch (start us, length us, event | category | flops | bytes accessed | tf_op | source)
XLA Modules:
  0.0 53.2 jit_solution(4239668422277529866)
XLA Ops:
  0.6 51.5 %log_linear.1 = (bf16[128,512]{1,0:T(8,128)(2,1)S(1)}, f32[512,128]{1,0:T(8,128)S(1)}, f32[512,128]{1,0:T(8,128)S(1)}, f32[512,128]{1,0:T(8,128)S(1)}, f32[512,128]{1,0:T(8,128)S(1)}) custom-call(f32[512,128]{1,0:T(8,128)} %bitcast.6, f32[512,128]{1,0:T(8,128)} %bitcast.7, f32[512,128]{1,0:T(8,128)} %bitcast.8, f32[7,4,128]{2,1,0:T(4,128)} %lam_h.1, ...), custom_call_target="tpu_custom_call" | custom-call | tf_op jit(solution)/shard_map/log_linear/pallas_call | solution.py:650
  52.2 1.1 %results.1 = (bf16[128,512]{1,0:T(8,128)(2,1)}, f32[512,128]{1,0:T(8,128)}, f32[512,128]{1,0:T(8,128)}, f32[512,128]{1,0:T(8,128)}, f32[512,128]{1,0:T(8,128)}) custom-call(bf16[128,512]{1,0:T(8,128)(2,1)S(1)} %get-tuple-element.15.refs_0_, f32[512,128]{1,0:T(8,128)S(1)} %get-tuple-element.16.refs_1_, f32[512,128]{1,0:T(8,128)S(1)} %get-tuple-element.17.refs_2_, ...), custom_call_target="tpu_custom_call" | custom-call | tf_op jit(solution)/shard_map/results/pallas_call | solution.py:684

commit v7 on v6

--- a/solution.py
+++ b/solution.py
@@ -421,7 +421,7 @@
         a16 = attf[h].astype(BF)
         att16[:, 128 * h : 128 * h + 128] = a16
         at[0, head(h), :] = a16.T
-        for j in (1, 3, 2):
+        for j in (2, 1, 3):
             send(at.at[0, head(h)], at.at[j, head(h)], ("at", h), d_y[j])
 
     @pl.when(place4 == 1)

time: 53.8 us -> 54 us (level)
  no operation moved by 1% of the time
where the time goes in v7:
time: 54 us; the launch traced here: 53.1 us
  Pallas kernels  52.5 us (97%)
  between operations  0.64 us (1%)
    pallas_call x1, Pallas kernels, body(): pl.pallas_call(body_kernel, out_shape=(jax.ShapeDtypeStruct((128, 512), B...  51.4 us

profile of v7, /device:TPU:8, one launch (start us, length us, event | category | flops | bytes accessed | tf_op | source)
XLA Modules:
  0.0 53.1 jit_solution(12521395466780504761)
XLA Ops:
  0.6 51.4 %log_linear.1 = (bf16[128,512]{1,0:T(8,128)(2,1)S(1)}, f32[512,128]{1,0:T(8,128)S(1)}, f32[512,128]{1,0:T(8,128)S(1)}, f32[512,128]{1,0:T(8,128)S(1)}, f32[512,128]{1,0:T(8,128)S(1)}) custom-call(f32[512,128]{1,0:T(8,128)} %bitcast.6, f32[512,128]{1,0:T(8,128)} %bitcast.7, f32[512,128]{1,0:T(8,128)} %bitcast.8, f32[7,4,128]{2,1,0:T(4,128)} %lam_h.1, ...), custom_call_target="tpu_custom_call" | custom-call | tf_op jit(solution)/shard_map/log_linear/pallas_call | solution.py:650
  52.1 1.1 %results.1 = (bf16[128,512]{1,0:T(8,128)(2,1)}, f32[512,128]{1,0:T(8,128)}, f32[512,128]{1,0:T(8,128)}, f32[512,128]{1,0:T(8,128)}, f32[512,128]{1,0:T(8,128)}) custom-call(bf16[128,512]{1,0:T(8,128)(2,1)S(1)} %get-tuple-element.15.refs_0_, f32[512,128]{1,0:T(8,128)S(1)} %get-tuple-element.16.refs_1_, f32[512,128]{1,0:T(8,128)S(1)} %get-tuple-element.17.refs_2_, ...), custom_call_target="tpu_custom_call" | custom-call | tf_op jit(solution)/shard_map/results/pallas_call | solution.py:684
